TPU v7x, 32 devices: a whole 2x2x4 slice. The times are simulated.
32 devices in a mesh: tile: 8 (over y, x, core), mode: 4 (over z).
Axes of the slice: x: 2, y: 2, z: 4, core: 2. Of those that a mesh axis runs over, the one named last changes fastest.
Arguments:
- object_tiles: float32 [8, 2, 2, 128, 128], P('tile'), may hold values from -1.5 to 1.5
- probe: float32 [16, 2, 128, 128], P('mode'), may hold values from -1 to 1
- propagator_phase: float32 [128, 128], replicated, may hold values from -3.140625 to 3.140625
- measured: float32 [32, 128, 128], P('tile'), may hold values from 0.25 to 2
- positions: int32 [32, 2], P('tile'), may hold values from 0 to 128, as said below
Outputs:
- updated_object: float32 [8, 2, 2, 128, 128], P('tile')
- intensity: float32 [32, 128, 128], P('tile')
Inputs may be any that keep to these rules, and one draw needn't show every extreme that they name: `positions`: row and column of the top-left cell of a pattern's 128 x 128 window within its tile's extended region.
All inputs are finite; a program needn't handle non-finite values.
Results may differ from a plain program's by a relative error of at most 0.0003.
Values sent between devices are 32-bit elements; how exact they have to be, the bound alone decides.
No kernel may reach another device: no remote copies, remote signals or barrier semaphores. Data moves between devices by JAX's collectives and lax.ppermute only.
A program may use at most 64 MiB of HBM per device.

v0:
```python
import math

import jax
import jax.numpy as jnp
import numpy as np
from jax import lax
from jax.experimental import pallas as pl
from jax.experimental.pallas import tpu as pltpu
from jax.sharding import PartitionSpec as P

HALO = 64
STEPS = 2
TILE_COLS = 8
SUB = 8

learning_rate = 0.5

f32 = jnp.float32
bf16 = jnp.bfloat16

VMEM = pl.BlockSpec(memory_space=pltpu.VMEM)
SMEM = pl.BlockSpec(memory_space=pltpu.SMEM)


def dft_matrix(order):
    index = np.arange(order)
    angle = (np.outer(index, index) % order) * (2.0 * math.pi / order)
    factor = 1.0 / math.sqrt(order)
    cos, sin = np.cos(angle) * factor, -np.sin(angle) * factor
    table = np.block([[cos, sin], [-sin, cos]])
    high = table.astype(bf16)
    low = (table - high.astype(np.float64)).astype(bf16)
    return np.stack([high, low])


def call(body, outs, args, scratch=(), mib=24):
    specs = [SMEM if a.dtype == jnp.int32 else VMEM for a in args]
    return pl.pallas_call(
        body,
        out_shape=[jax.ShapeDtypeStruct(s, f32) for s in outs],
        in_specs=specs,
        out_specs=[VMEM] * len(outs),
        scratch_shapes=list(scratch),
        compiler_params=pltpu.CompilerParams(vmem_limit_bytes=mib << 20),
    )(*args)


def halves(x):
    high = x.astype(bf16)
    return high, (x - high.astype(f32)).astype(bf16)


def product(x, high, low):
    xh, xl = halves(x)
    dot = lambda a, b: jnp.dot(a, b, preferred_element_type=f32)
    return dot(xh, high) + dot(xl, high) + dot(xh, low)


def flip(x, k):
    rows = []
    for i in range(x.shape[0] // k):
        part = x[i * k : (i + 1) * k]
        rows.append(jnp.concatenate([part[:, :k].T, part[:, k:].T], axis=1))
    return jnp.concatenate(rows, axis=0)


def dft(waves, high, low):
    k = waves[0].shape[0]
    x = jnp.concatenate(waves, axis=0)
    y = product(flip(product(x, high, low), k), high, low)
    return [y[i * k : (i + 1) * k] for i in range(len(waves))]


def pair(re, im):
    return jnp.concatenate([re, im], axis=1)


def window(plane, row, col, k):
    tall, width = k + SUB, plane.shape[1]
    base = pl.multiple_of(row - row % SUB, SUB)
    part = pltpu.roll(plane[pl.ds(base, tall), :], (width - col) % width, 1)[:, :k]
    return pltpu.roll(part, (tall - row % SUB) % tall, 0)[:k]


def add_window(ext, value, row, col):
    k, width = value.shape[0], ext.shape[1]
    wide = pltpu.roll(pair(value, jnp.zeros((k, width - k), f32)), col, 1)
    tall = jnp.concatenate([wide, jnp.zeros((SUB, width), f32)], axis=0)
    where = pl.ds(pl.multiple_of(row - row % SUB, SUB), k + SUB)
    ext[where, :] = ext[where, :] + pltpu.roll(tall, row % SUB, 0)


def forward_modes(windows, probes, cos_t, sin_t, table, u_outs, psi_outs, k):
    high, low = table[0], table[1]
    ar, ai, br, bi = [windows(p) for p in range(4)]
    ar, br = 1.0 + ar, 1.0 + br
    total = jnp.zeros((k, k), f32)
    for probe, u_out, psi_out in zip(probes, u_outs, psi_outs):
        count = probe.shape[0]
        waves = []
        for m in range(count):
            pr, pi = probe[m, 0], probe[m, 1]
            waves.append(pair(ar * pr - ai * pi, ar * pi + ai * pr))
        turned = []
        for s in dft(waves, high, low):
            sr, si = s[:, :k], s[:, k:]
            turned.append(pair(cos_t * sr - sin_t * si, -(cos_t * si + sin_t * sr)))
        waves = []
        for m, u in enumerate(dft(turned, high, low)):
            u_out[m] = u
            ur, ui = u[:, :k], u[:, k:]
            waves.append(pair(br * ur + bi * ui, bi * ur - br * ui))
        for m, psi in enumerate(dft(waves, high, low)):
            psi_out[m] = psi
            square = psi * psi
            total = total + (square[:, :k] + square[:, k:])
    return total.T


def first_forward(step_rows, rows):
    def body(z_ref, pos, *refs):
        if rows:
            ext_ref, probe, cos_t, sin_t, table = refs[:5]
            win, owned, part, u_out, psi_out, ext = refs[5:]
            ext[...] = ext_ref[...]
        else:
            tile, left, right, probe, cos_t, sin_t, table = refs[:7]
            win, owned, part, u_out, psi_out, ext = refs[7:]
            planes, core = tile.shape[0], tile.shape[1]
            ext[...] = jnp.zeros(ext.shape, f32)
            for p in range(planes):
                ext[p, HALO : HALO + core, :] = jnp.concatenate(
                    [left[p][:, core - HALO :], tile[p], right[p][:, :HALO]], axis=1
                )
        planes, k = win.shape[0], win.shape[1]
        z = z_ref[0]
        q = z % step_rows
        row, col = pos[q, 0], pos[q, 1]
        for p in range(planes):
            win[p] = window(ext.at[p], row, col, k)
        owned[...] = ext[z]
        part[...] = forward_modes(
            lambda p: win[p], [probe], cos_t[...], sin_t[...], table, [u_out], [psi_out], k
        )

    return body


def more_forward(win, probe, cos_t, sin_t, table, before, part, u_out, psi_out):
    k = win.shape[1]
    part[...] = before[...] + forward_modes(
        lambda p: win[p], [probe], cos_t[...], sin_t[...], table, [u_out], [psi_out], k
    )


def next_forward(count):
    def body(z_ref, *refs):
        pieces, refs = refs[:count], refs[count:]
        probe_a, probe_b, cos_t, sin_t, table, win, part, u_a, psi_a, u_b, psi_b = refs
        z = z_ref[0]
        k = win.shape[1]
        for j, piece in enumerate(pieces):
            win[(z + count - j) % count] = piece[...]
        part[...] = forward_modes(
            lambda p: win[p], [probe_a, probe_b], cos_t[...], sin_t[...], table,
            [u_a, u_b], [psi_a, psi_b], k,
        )

    return body


def backward(step, step_rows, parts, count):
    def body(z_ref, *refs):
        partials, refs = refs[:parts], refs[parts:]
        measured, win, probe_a, probe_b, u_a, psi_a, u_b, psi_b, cos_t, sin_t, table = refs[:11]
        intensity, sends, grads = refs[11], refs[12 : 12 + count], refs[12 + count]
        z = z_ref[0]
        k = win.shape[1]
        high, low = table[0], table[1]
        cos, sin = cos_t[...], sin_t[...]
        total = partials[0][...]
        for extra in partials[1:]:
            total = total + extra[...]
        intensity[...] = total
        twice = (2.0 * (total - measured[step * step_rows + z % step_rows])).T
        br, bi = 1.0 + win[2], win[3]
        zero = jnp.zeros((k, k), f32)
        g0r, g0i, g1r, g1i = zero, zero, zero, zero
        for probe, u_in, psi_in in ((probe_a, u_a, psi_a), (probe_b, u_b, psi_b)):
            modes = probe.shape[0]
            waves = []
            for m in range(modes):
                psi = psi_in[m]
                waves.append(pair(twice * psi[:, :k], -(twice * psi[:, k:])))
            turned = []
            for m, g in enumerate(dft(waves, high, low)):
                gr, gi = g[:, :k], -g[:, k:]
                u = u_in[m]
                ur, ui = u[:, :k], u[:, k:]
                g1r = g1r + (ur * gr - ui * gi)
                g1i = g1i + (ur * gi + ui * gr)
                turned.append(pair(br * gr + bi * gi, br * gi - bi * gr))
            waves = []
            for s in dft(turned, high, low):
                sr, si = s[:, :k], s[:, k:]
                waves.append(pair(cos * sr + sin * si, sin * sr - cos * si))
            for m, g in enumerate(dft(waves, high, low)):
                gr, gi = g[:, :k], -g[:, k:]
                pr, pi = probe[m, 0], probe[m, 1]
                g0r = g0r + (pr * gr + pi * gi)
                g0i = g0i + (pr * gi - pi * gr)
        grads[0], grads[1], grads[2], grads[3] = g0r, g0i, g1r, g1i
        for j in range(count):
            sends[j][...] = grads[(z + j) % count]

    return body


def scatter(step, step_rows, count, rows):
    def body(z_ref, pos, *refs):
        pieces, outs, ext = refs[:count], refs[count:-1], refs[-1]
        z = z_ref[0]
        q = z % step_rows
        width = ext.shape[1]
        ext[...] = jnp.zeros(ext.shape, f32)
        for i in range(step_rows):
            total = pieces[i][...]
            for j in range(i + step_rows, count, step_rows):
                total = total + pieces[j][...]
            which = step * step_rows + (q + step_rows - i) % step_rows
            add_window(ext, total, pos[which, 0], pos[which, 1])
        if rows:
            outs[0][...] = ext[...]
        else:
            half = width // 2
            core = outs[0].shape[0]
            outs[0][...] = ext[HALO : HALO + core, :half]
            outs[1][...] = ext[HALO : HALO + core, half:]

    return body


def updated_rows(left, right, from_left, from_right, owned):
    grad = pair(left[...] + from_left[...], right[...] + from_right[...])
    return owned[HALO : HALO + grad.shape[0], :] - learning_rate * grad


def next_windows(step, step_rows, source, z, pos, outs):
    q = z % step_rows
    k = outs[0].shape[0]
    for i, out in enumerate(outs):
        which = step * step_rows + (q + i) % step_rows
        row, col = pos[which, 0], pos[which, 1]
        out[...] = window(source, row, col, k)


def update(step, step_rows):
    def body(z_ref, pos, left, right, from_left, from_right, owned, fresh, *outs):
        fresh[...] = jnp.zeros(fresh.shape, f32)
        fresh[HALO : HALO + left.shape[0], :] = updated_rows(left, right, from_left, from_right, owned)
        next_windows(step, step_rows, fresh, z_ref[0], pos, outs)

    return body


def update_middle(left, right, from_left, from_right, owned, middle):
    middle[...] = updated_rows(left, right, from_left, from_right, owned)


def only_windows(step, step_rows):
    def body(z_ref, pos, owned, *outs):
        next_windows(step, step_rows, owned, z_ref[0], pos, outs)

    return body


def last_update(left, right, from_left, from_right, owned, core):
    middle = updated_rows(left, right, from_left, from_right, owned)
    core[...] = middle[:, HALO : middle.shape[1] - HALO]


def gather_planes(count):
    def body(z_ref, *refs):
        out = refs[count]
        for j in range(count):
            out[(z_ref[0] + count - j) % count] = refs[j][...]

    return body


def gather_intensities(step_rows):
    def body(z_ref, *refs):
        out = refs[-1]
        q = z_ref[0] % step_rows
        for i, ref in enumerate(refs[:-1]):
            step, j = divmod(i, step_rows)
            out[step * step_rows + (q + step_rows - j) % step_rows] = ref[...]

    return body


def ring(axis, steps):
    count = lax.axis_size(axis)
    return [(i, (i + steps) % count) for i in range(count)]


def shift(value, axis, steps):
    return lax.ppermute(value, axis, ring(axis, steps))


def from_behind(value, axis, steps):
    count = lax.axis_size(axis)
    first, last = (max(0, -steps), min(count, count - steps))
    return lax.ppermute(value, axis, [(source, source + steps) for source in range(first, last)])


def within(value, axis, group, steps):
    count = lax.axis_size(axis)
    pairs = [(i, i - i % group + (i % group + steps) % group) for i in range(count)]
    return lax.ppermute(value, axis, pairs)


def local(object_tiles, probe, propagator_phase, measured, positions):
    layers, core = object_tiles.shape[1], object_tiles.shape[3]
    count = layers * 2
    k = probe.shape[-1]
    modes = probe.shape[0]
    step_rows = positions.shape[0] // STEPS
    group = lax.axis_size("mode")
    assert layers == 2 and count == group and step_rows == 2 and core == 2 * HALO
    rows = lax.axis_size("tile") > TILE_COLS
    extent = core + 2 * HALO
    tall = (extent + SUB, extent)
    z = lax.axis_index("mode").astype(jnp.int32).reshape(1)
    planes = object_tiles.reshape(count, core, core)
    flat, wave = (k, k), (modes, k, 2 * k)

    other_probe = within(probe, "mode", step_rows, 1)
    from_left = shift(planes, "tile", 1)
    from_right = shift(planes, "tile", -1)
    cos_t, sin_t = jnp.cos(propagator_phase.T), jnp.sin(propagator_phase.T)
    table = jnp.asarray(dft_matrix(k))
    optics = (cos_t, sin_t, table)

    if rows:
        wide = jnp.concatenate(
            [from_left[:, :, core - HALO :], planes, from_right[:, :, :HALO]], axis=2
        )
        above = from_behind(wide[:, core - HALO :], "tile", TILE_COLS)
        below = from_behind(wide[:, :HALO], "tile", -TILE_COLS)
        slack = jnp.zeros((count, SUB, extent), f32)
        objects = (jnp.concatenate([above, wide, below, slack], axis=1),)
    else:
        objects = (planes, from_left, from_right)

    win, owned, part, u_a, psi_a = call(
        first_forward(step_rows, rows),
        [(count, k, k), tall, flat, wave, wave],
        (z, positions) + objects + (probe,) + optics,
        [pltpu.VMEM((count,) + tall, f32)],
    )
    part, u_b, psi_b = call(
        more_forward, [flat, wave, wave], (win, other_probe) + optics + (part,)
    )

    kept = []
    for step in range(STEPS):
        partials = [part] + [shift(part, "mode", j) for j in range(step_rows, group, step_rows)]
        out = call(
            backward(step, step_rows, len(partials), count),
            [flat] * (1 + count),
            (z,) + tuple(partials) + (measured, win, probe, other_probe, u_a, psi_a, u_b, psi_b) + optics,
            [pltpu.VMEM((count, k, k), f32)],
        )
        intensity, sends = out[0], out[1:]
        kept.append(intensity)
        kept.extend(within(intensity, "mode", step_rows, j) for j in range(1, step_rows))
        pieces = [sends[0]] + [shift(sends[j], "mode", j) for j in range(1, group)]
        half = (core, extent // 2)
        grads = call(
            scatter(step, step_rows, count, rows),
            [tall] if rows else [half, half],
            (z, positions) + tuple(pieces),
            [pltpu.VMEM(tall, f32)],
        )
        if rows:
            whole = grads[0]
            middle = whole[HALO : HALO + core]
            middle = middle.at[core - HALO :].add(from_behind(whole[:HALO], "tile", -TILE_COLS))
            middle = middle.at[:HALO].add(from_behind(whole[HALO + core : extent], "tile", TILE_COLS))
            grads = [middle[:, : extent // 2], middle[:, extent // 2 :]]
        left, right = grads
        sums = (left, right, shift(right, "tile", 1), shift(left, "tile", -1), owned)
        if step + 1 == STEPS:
            break
        if rows:
            (middle,) = call(update_middle, [(core, extent)], sums)
            above = from_behind(middle[core - HALO :], "tile", TILE_COLS)
            below = from_behind(middle[:HALO], "tile", -TILE_COLS)
            slack = jnp.zeros((SUB, extent), f32)
            owned = jnp.concatenate([above, middle, below, slack], axis=0)
            outs = call(only_windows(step + 1, step_rows), [flat] * step_rows, (z, positions, owned))
        else:
            out = call(
                update(step + 1, step_rows),
                [tall] + [flat] * step_rows,
                (z, positions) + sums,
            )
            owned, outs = out[0], out[1:]
        pieces = [outs[0]] + [shift(outs[j % step_rows], "mode", j) for j in range(1, group)]
        win, part, u_a, psi_a, u_b, psi_b = call(
            next_forward(count),
            [(count, k, k), flat, wave, wave, wave, wave],
            (z,) + tuple(pieces) + (probe, other_probe) + optics,
        )

    (plane,) = call(last_update, [(core, core)], sums)
    pieces = [plane] + [shift(plane, "mode", j) for j in range(1, group)]
    (updated,) = call(gather_planes(count), [(count, core, core)], (z,) + tuple(pieces))
    (intensities,) = call(gather_intensities(step_rows), [measured.shape], (z,) + tuple(kept))
    return (updated.reshape(object_tiles.shape), intensities)


def solution(mesh):
    return jax.shard_map(
        local,
        mesh=mesh,
        in_specs=(
            P("tile", None, None, None, None),
            P("mode", None, None, None),
            P(),
            P("tile", None, None),
            P("tile", None),
        ),
        out_specs=(P("tile", None, None, None, None), P("tile", None, None)),
        check_vma=False,
    )
```

profile of v0, /device:TPU:0, one launch (start us, length us, event | category | flops | bytes accessed | tf_op | source)
XLA Modules:
  0.0 96.3 jit_solution(2083808362463503778)
XLA Ops:
  0.6 0.0 copy-start.2
  0.6 3.1 %collective-permute-start.2 = (f32[4,2,128,128]{3,2,1,0:T(8,128)}, f32[4,2,128,128]{3,2,1,0:T(8,128)S(1)}, u32[]{:S(2)}, u32[]{:S(2)}) collective-permute-start(f32[4,2,128,128]{3,2,1,0:T(8,128)} %refs_4_.5), channel_id=1, source_target_pairs={{0,1},{1,0},{2,3},{3,2},{4,5},{5,4},{6,7},{7,6},{8,9},{9,8},{10,11... | collective-permute-start | bytes 1572872 | tf_op jit(solution)/shard_map/ppermute | solution.py:320
  3.8 0.0 collective-permute-start
  3.8 2.6 %collective-permute-start.1 = (f32[4,128,128]{2,1,0:T(8,128)}, f32[4,128,128]{2,1,0:T(8,128)S(1)}, u32[]{:S(2)}, u32[]{:S(2)}) collective-permute-start(f32[4,128,128]{2,1,0:T(8,128)} %bitcast.8), channel_id=1, source_target_pairs={{0,28},{4,0},{8,4},{12,8},{16,12},{20,16},{24,20},{28,24},{1,29},{... | collective-permute-start | bytes 786440 | tf_op jit(solution)/shard_map/ppermute | solution.py:308
  6.4 0.9 copy.8
  7.3 0.8 copy.13.pos
  8.1 0.2 sine_bitcast_fusion
  8.3 3.3 %collective-permute-done.refs_1_ = f32[4,128,128]{2,1,0:T(8,128)S(1)} collective-permute-done((f32[4,128,128]{2,1,0:T(8,128)}, f32[4,128,128]{2,1,0:T(8,128)S(1)}, u32[]{:S(2)}, u32[]{:S(2)}) %collective-permute-start) | collective-permute-done | bytes 262176 | tf_op jit(solution)/shard_map/ppermute | solution.py:308
  11.6 0.1 collective-permute-done.1.refs_2_
  11.7 1.0 %copy-done = f32[4,2,128,128]{3,2,1,0:T(8,128)S(1)} copy-done((f32[4,2,128,128]{3,2,1,0:T(8,128)S(1)}, f32[4,2,128,128]{3,2,1,0:T(8,128)}, u32[]{:S(2)}) %copy-start) | copy-done | bytes 524312
  12.7 0.9 copy-done.4
  13.7 3.8 %shard_map.77 = (f32[4,128,128]{2,1,0:T(8,128)S(1)}, f32[264,256]{1,0:T(8,128)S(1)}, f32[128,128]{1,0:T(8,128)S(1)}, f32[4,128,256]{2,1,0:T(8,128)S(1)}, f32[4,128,256]{2,1,0:T(8,128)S(1)}) custom-call(s32[1]{0:T(128)} %bitcast.z_ref, s32[4,2]{1,0:T(4,128)S(1)} %copy.13.pos, f32[4,128,128]{2,1,0:T(8,128)S(1)} %bitcast.9, ...), custom_call_target="tpu_custom_call" | custom-call | tf_op jit(solution)/shard_map/pallas_call | solution.py:38
  17.4 0.0 collective-permute-done.2.probe.refs_5_
  17.5 0.0 copy-start.1
  17.5 0.0 copy-start.3
  17.5 2.8 %shard_map.78 = (f32[128,128]{1,0:T(8,128)S(1)}, f32[4,128,256]{2,1,0:T(8,128)S(1)}, f32[4,128,256]{2,1,0:T(8,128)S(1)}) custom-call(f32[4,128,128]{2,1,0:T(8,128)S(1)} %get-tuple-element.33.win.refs_3_, f32[4,2,128,128]{3,2,1,0:T(8,128)S(1)} %collective-permute-done.2.probe.refs_5_, f32[128,128]{1,0:T(8,128)S(1)} %get-tuple-element.65.refs_4_.cos_t.refs_10_.refs_6_, ...), custom_call_target="tpu_custom_call" | custom-call | tf_op jit(solution)/shard_map/pallas_call | solution.py:38
  20.3 2.7 %collective-permute-start.3 = (f32[128,128]{1,0:T(8,128)S(1)}, f32[128,128]{1,0:T(8,128)S(1)}, u32[]{:S(2)}, u32[]{:S(2)}) collective-permute-start(f32[128,128]{1,0:T(8,128)S(1)} %get-tuple-element.35.refs_0_), channel_id=1, source_target_pairs={{0,2},{1,3},{2,0},{3,1},{4,6},{5,7},{6,4},{7,5},{8,10},{9,11},{10,... | collective-permute-start | bytes 196616 | tf_op jit(solution)/shard_map/ppermute | solution.py:308
  22.9 4.3 %collective-permute-done.3.refs_1_ = f32[128,128]{1,0:T(8,128)S(1)} collective-permute-done((f32[128,128]{1,0:T(8,128)S(1)}, f32[128,128]{1,0:T(8,128)S(1)}, u32[]{:S(2)}, u32[]{:S(2)}) %collective-permute-start.3) | collective-permute-done | bytes 65568 | tf_op jit(solution)/shard_map/ppermute | solution.py:308
  27.2 5.1 %shard_map.79 = (f32[128,128]{1,0:T(8,128)S(1)}, f32[128,128]{1,0:T(8,128)S(1)}, f32[128,128]{1,0:T(8,128)S(1)}, f32[128,128]{1,0:T(8,128)S(1)}, f32[128,128]{1,0:T(8,128)S(1)}) custom-call(s32[1]{0:T(128)} %bitcast.z_ref, f32[128,128]{1,0:T(8,128)S(1)} %get-tuple-element.35.refs_0_, f32[128,128]{1,0:T(8,128)S(1)} %collective-permute-done.3.refs_1_, ...), custom_call_target="tpu_custom_call" | custom-call | tf_op jit(solution)/shard_map/pallas_call | solution.py:38
  32.3 0.1 collective-permute-start.4
  32.4 1.3 %collective-permute-start.5 = (f32[128,128]{1,0:T(8,128)S(1)}, f32[128,128]{1,0:T(8,128)S(1)}, u32[]{:S(2)}, u32[]{:S(2)}) collective-permute-start(f32[128,128]{1,0:T(8,128)S(1)} %get-tuple-element.42), channel_id=1, source_target_pairs={{0,2},{1,3},{2,0},{3,1},{4,6},{5,7},{6,4},{7,5},{8,10},{9,11},{10,... | collective-permute-start | bytes 196616 | tf_op jit(solution)/shard_map/ppermute | solution.py:308
  33.7 2.6 %collective-permute-start.6 = (f32[128,128]{1,0:T(8,128)S(1)}, f32[128,128]{1,0:T(8,128)S(1)}, u32[]{:S(2)}, u32[]{:S(2)}) collective-permute-start(f32[128,128]{1,0:T(8,128)S(1)} %get-tuple-element.43), channel_id=1, source_target_pairs={{0,3},{1,0},{2,1},{3,2},{4,7},{5,4},{6,5},{7,6},{8,11},{9,8},{10,9... | collective-permute-start | bytes 196616 | tf_op jit(solution)/shard_map/ppermute | solution.py:308
  36.3 3.0 %collective-permute-done.4.refs_1_ = f32[128,128]{1,0:T(8,128)S(1)} collective-permute-done((f32[128,128]{1,0:T(8,128)S(1)}, f32[128,128]{1,0:T(8,128)S(1)}, u32[]{:S(2)}, u32[]{:S(2)}) %collective-permute-start.4) | collective-permute-done | bytes 65568 | tf_op jit(solution)/shard_map/ppermute | solution.py:308
  39.3 1.8 %collective-permute-done.5.refs_2_ = f32[128,128]{1,0:T(8,128)S(1)} collective-permute-done((f32[128,128]{1,0:T(8,128)S(1)}, f32[128,128]{1,0:T(8,128)S(1)}, u32[]{:S(2)}, u32[]{:S(2)}) %collective-permute-start.5) | collective-permute-done | bytes 65568 | tf_op jit(solution)/shard_map/ppermute | solution.py:308
  41.1 0.0 collective-permute-done.6.refs_3_
  41.1 0.8 shard_map.80
  41.9 0.1 collective-permute-start.7
  42.0 2.6 %collective-permute-start.8 = (f32[128,128]{1,0:T(8,128)S(1)}, f32[128,128]{1,0:T(8,128)S(1)}, u32[]{:S(2)}, u32[]{:S(2)}) collective-permute-start(f32[128,128]{1,0:T(8,128)S(1)} %get-tuple-element.44.left), channel_id=1, source_target_pairs={{0,28},{4,0},{8,4},{12,8},{16,12},{20,16},{24,20},{28,24},{1,29},{... | collective-permute-start | bytes 196616 | tf_op jit(solution)/shard_map/ppermute | solution.py:308
  44.6 1.9 %collective-permute-done.7.from_left = f32[128,128]{1,0:T(8,128)S(1)} collective-permute-done((f32[128,128]{1,0:T(8,128)S(1)}, f32[128,128]{1,0:T(8,128)S(1)}, u32[]{:S(2)}, u32[]{:S(2)}) %collective-permute-start.7) | collective-permute-done | bytes 65568 | tf_op jit(solution)/shard_map/ppermute | solution.py:308
  46.5 0.0 collective-permute-done.8.from_right
  46.5 0.7 shard_map.81
  47.3 0.7 collective-permute-start.10
  47.9 3.3 %collective-permute-start.11 = (f32[128,128]{1,0:T(8,128)S(1)}, f32[128,128]{1,0:T(8,128)S(1)}, u32[]{:S(2)}, u32[]{:S(2)}) collective-permute-start(f32[128,128]{1,0:T(8,128)S(1)} %get-tuple-element.48), channel_id=1, source_target_pairs={{0,3},{1,0},{2,1},{3,2},{4,7},{5,4},{6,5},{7,6},{8,11},{9,8},{10,9... | collective-permute-start | bytes 196616 | tf_op jit(solution)/shard_map/ppermute | solution.py:308
  51.3 0.0 collective-permute-start.9
  51.3 3.4 %collective-permute-done.10.refs_2_ = f32[128,128]{1,0:T(8,128)S(1)} collective-permute-done((f32[128,128]{1,0:T(8,128)S(1)}, f32[128,128]{1,0:T(8,128)S(1)}, u32[]{:S(2)}, u32[]{:S(2)}) %collective-permute-start.10) | collective-permute-done | bytes 65568 | tf_op jit(solution)/shard_map/ppermute | solution.py:308
  54.6 0.0 collective-permute-done.11.refs_3_
  54.6 2.7 %collective-permute-done.9.refs_1_ = f32[128,128]{1,0:T(8,128)S(1)} collective-permute-done((f32[128,128]{1,0:T(8,128)S(1)}, f32[128,128]{1,0:T(8,128)S(1)}, u32[]{:S(2)}, u32[]{:S(2)}) %collective-permute-start.9) | collective-permute-done | bytes 65568 | tf_op jit(solution)/shard_map/ppermute | solution.py:308
  57.3 4.9 %shard_map.82 = (f32[4,128,128]{2,1,0:T(8,128)S(1)}, f32[128,128]{1,0:T(8,128)S(1)}, f32[4,128,256]{2,1,0:T(8,128)S(1)}, f32[4,128,256]{2,1,0:T(8,128)S(1)}, f32...) custom-call(s32[1]{0:T(128)} %bitcast.z_ref, f32[128,128]{1,0:T(8,128)S(1)} %get-tuple-element.47.refs_0_, ...), custom_call_target="tpu_custom_call" | custom-call | tf_op jit(solution)/shard_map/pallas_call | solution.py:38
  62.3 0.8 collective-permute-start.12
  63.0 4.5 %collective-permute-done.12.refs_1_ = f32[128,128]{1,0:T(8,128)S(1)} collective-permute-done((f32[128,128]{1,0:T(8,128)S(1)}, f32[128,128]{1,0:T(8,128)S(1)}, u32[]{:S(2)}, u32[]{:S(2)}) %collective-permute-start.12) | collective-permute-done | bytes 65568 | tf_op jit(solution)/shard_map/ppermute | solution.py:308
  67.5 5.1 %shard_map.83 = (f32[128,128]{1,0:T(8,128)S(1)}, f32[128,128]{1,0:T(8,128)S(1)}, f32[128,128]{1,0:T(8,128)S(1)}, f32[128,128]{1,0:T(8,128)S(1)}, f32[128,128]{1,0:T(8,128)S(1)}) custom-call(s32[1]{0:T(128)} %bitcast.z_ref, f32[128,128]{1,0:T(8,128)S(1)} %get-tuple-element.49.refs_0_, f32[128,128]{1,0:T(8,128)S(1)} %collective-permute-done.12.refs_1_, ...), custom_call_target="tpu_custom_call" | custom-call | tf_op jit(solution)/shard_map/pallas_call | solution.py:38
  72.6 0.1 collective-permute-start.13
  72.7 2.9 %collective-permute-start.14 = (f32[128,128]{1,0:T(8,128)S(1)}, f32[128,128]{1,0:T(8,128)S(1)}, u32[]{:S(2)}, u32[]{:S(2)}) collective-permute-start(f32[128,128]{1,0:T(8,128)S(1)} %get-tuple-element.57), channel_id=1, source_target_pairs={{0,2},{1,3},{2,0},{3,1},{4,6},{5,7},{6,4},{7,5},{8,10},{9,11},{10,... | collective-permute-start | bytes 196616 | tf_op jit(solution)/shard_map/ppermute | solution.py:308
  75.6 0.9 collective-permute-start.15
  76.5 2.3 %collective-permute-done.13.refs_1_ = f32[128,128]{1,0:T(8,128)S(1)} collective-permute-done((f32[128,128]{1,0:T(8,128)S(1)}, f32[128,128]{1,0:T(8,128)S(1)}, u32[]{:S(2)}, u32[]{:S(2)}) %collective-permute-start.13) | collective-permute-done | bytes 65568 | tf_op jit(solution)/shard_map/ppermute | solution.py:308
  78.8 1.2 %collective-permute-done.14.refs_2_ = f32[128,128]{1,0:T(8,128)S(1)} collective-permute-done((f32[128,128]{1,0:T(8,128)S(1)}, f32[128,128]{1,0:T(8,128)S(1)}, u32[]{:S(2)}, u32[]{:S(2)}) %collective-permute-start.14) | collective-permute-done | bytes 65568 | tf_op jit(solution)/shard_map/ppermute | solution.py:308
  80.0 0.4 collective-permute-done.15.refs_3_
  80.4 0.8 shard_map.84
  81.1 0.1 collective-permute-start.16
  81.2 2.6 %collective-permute-start.17 = (f32[128,128]{1,0:T(8,128)S(1)}, f32[128,128]{1,0:T(8,128)S(1)}, u32[]{:S(2)}, u32[]{:S(2)}) collective-permute-start(f32[128,128]{1,0:T(8,128)S(1)} %get-tuple-element.59.left), channel_id=1, source_target_pairs={{0,28},{4,0},{8,4},{12,8},{16,12},{20,16},{24,20},{28,24},{1,29},{... | collective-permute-start | bytes 196616 | tf_op jit(solution)/shard_map/ppermute | solution.py:308
  83.8 1.3 %collective-permute-start.21 = (f32[128,128]{1,0:T(8,128)S(1)}, f32[128,128]{1,0:T(8,128)S(1)}, u32[]{:S(2)}, u32[]{:S(2)}) collective-permute-start(f32[128,128]{1,0:T(8,128)S(1)} %get-tuple-element.62.refs_0_), channel_id=1, source_target_pairs={{0,1},{1,0},{2,3},{3,2},{4,5},{5,4},{6,7},{7,6},{8,9},{9,8},{10,11... | collective-permute-start | bytes 196616 | tf_op jit(solution)/shard_map/ppermute | solution.py:320
  85.1 0.8 collective-permute-start.22
  85.9 0.0 collective-permute-done.16.from_left
  85.9 0.1 shard_map.85.refs_0_
  86.0 1.3 %collective-permute-start.18 = (f32[128,128]{1,0:T(8,128)S(1)}, f32[128,128]{1,0:T(8,128)S(1)}, u32[]{:S(2)}, u32[]{:S(2)}) collective-permute-start(f32[128,128]{1,0:T(8,128)S(1)} %shard_map.85.refs_0_), channel_id=1, source_target_pairs={{0,1},{1,2},{2,3},{3,0},{4,5},{5,6},{6,7},{7,4},{8,9},{9,10},{10,1... | collective-permute-start | bytes 196616 | tf_op jit(solution)/shard_map/ppermute | solution.py:308
  87.3 2.0 %collective-permute-start.19 = (f32[128,128]{1,0:T(8,128)S(1)}, f32[128,128]{1,0:T(8,128)S(1)}, u32[]{:S(2)}, u32[]{:S(2)}) collective-permute-start(f32[128,128]{1,0:T(8,128)S(1)} %shard_map.85.refs_0_), channel_id=1, source_target_pairs={{0,2},{1,3},{2,0},{3,1},{4,6},{5,7},{6,4},{7,5},{8,10},{9,11},{10,... | collective-permute-start | bytes 196616 | tf_op jit(solution)/shard_map/ppermute | solution.py:308
  89.3 0.9 collective-permute-start.20
  90.2 0.0 collective-permute-done.21.refs_1_
  90.2 0.0 collective-permute-done.22.refs_3_
  90.2 0.7 shard_map.87
  90.9 1.8 %collective-permute-done.18.refs_1_ = f32[128,128]{1,0:T(8,128)S(1)} collective-permute-done((f32[128,128]{1,0:T(8,128)S(1)}, f32[128,128]{1,0:T(8,128)S(1)}, u32[]{:S(2)}, u32[]{:S(2)}) %collective-permute-start.18) | collective-permute-done | bytes 65568 | tf_op jit(solution)/shard_map/ppermute | solution.py:308
  92.7 2.9 %collective-permute-done.19.refs_2_ = f32[128,128]{1,0:T(8,128)S(1)} collective-permute-done((f32[128,128]{1,0:T(8,128)S(1)}, f32[128,128]{1,0:T(8,128)S(1)}, u32[]{:S(2)}, u32[]{:S(2)}) %collective-permute-start.19) | collective-permute-done | bytes 65568 | tf_op jit(solution)/shard_map/ppermute | solution.py:308
  95.6 0.0 collective-permute-done.20.refs_3_
  95.6 0.7 shard_map.86
  (6 shorter events, 0.0 us)
Async XLA Ops:
  0.6 11.1 %copy-start.2 = (bf16[2,256,256]{2,1,0:T(8,128)(2,1)S(1)}, bf16[2,256,256]{2,1,0:T(8,128)(2,1)}, u32[]{:S(2)}) copy-start(bf16[2,256,256]{2,1,0:T(8,128)(2,1)} %constant.6.clone.refs_6_.table.refs_12_.refs_8_) | copy-start | bytes 786436
  0.6 16.8 %collective-permute-start.2 = (f32[4,2,128,128]{3,2,1,0:T(8,128)}, f32[4,2,128,128]{3,2,1,0:T(8,128)S(1)}, u32[]{:S(2)}, u32[]{:S(2)}) collective-permute-start(f32[4,2,128,128]{3,2,1,0:T(8,128)} %refs_4_.5), channel_id=1, source_target_pairs={{0,1},{1,0},{2,3},{3,2},{4,5},{5,4},{6,7},{7,6},{8,9},{9,8},{10,11... | collective-permute-start | bytes 1572872 | tf_op jit(solution)/shard_map/ppermute | solution.py:320
  3.8 7.9 %collective-permute-start = (f32[4,128,128]{2,1,0:T(8,128)}, f32[4,128,128]{2,1,0:T(8,128)S(1)}, u32[]{:S(2)}, u32[]{:S(2)}) collective-permute-start(f32[4,128,128]{2,1,0:T(8,128)} %bitcast.7), channel_id=1, source_target_pairs={{0,4},{4,8},{8,12},{12,16},{16,20},{20,24},{24,28},{28,0},{1,5},{5... | collective-permute-start | bytes 786440 | tf_op jit(solution)/shard_map/ppermute | solution.py:308
  3.8 7.9 %collective-permute-start.1 = (f32[4,128,128]{2,1,0:T(8,128)}, f32[4,128,128]{2,1,0:T(8,128)S(1)}, u32[]{:S(2)}, u32[]{:S(2)}) collective-permute-start(f32[4,128,128]{2,1,0:T(8,128)} %bitcast.8), channel_id=1, source_target_pairs={{0,28},{4,0},{8,4},{12,8},{16,12},{20,16},{24,20},{28,24},{1,29},{... | collective-permute-start | bytes 786440 | tf_op jit(solution)/shard_map/ppermute | solution.py:308
  11.7 1.0 %copy-start = (f32[4,2,128,128]{3,2,1,0:T(8,128)S(1)}, f32[4,2,128,128]{3,2,1,0:T(8,128)}, u32[]{:S(2)}) copy-start(f32[4,2,128,128]{3,2,1,0:T(8,128)} %refs_4_.5) | copy-start | bytes 1572868
  12.7 0.9 copy-start.4
  17.5 9.8 %copy-start.1 = (f32[4,2,128,128]{3,2,1,0:T(8,128)S(1)}, f32[4,2,128,128]{3,2,1,0:T(8,128)}, u32[]{:S(2)}) copy-start(f32[4,2,128,128]{3,2,1,0:T(8,128)} %refs_4_.5) | copy-start | bytes 1572868
  17.5 9.8 %copy-start.3 = (f32[4,128,128]{2,1,0:T(8,128)S(1)}, f32[4,128,128]{2,1,0:T(8,128)}, u32[]{:S(2)}) copy-start(f32[4,128,128]{2,1,0:T(8,128)} %refs_2_.3) | copy-start | bytes 786436
  20.3 6.9 %collective-permute-start.3 = (f32[128,128]{1,0:T(8,128)S(1)}, f32[128,128]{1,0:T(8,128)S(1)}, u32[]{:S(2)}, u32[]{:S(2)}) collective-permute-start(f32[128,128]{1,0:T(8,128)S(1)} %get-tuple-element.35.refs_0_), channel_id=1, source_target_pairs={{0,2},{1,3},{2,0},{3,1},{4,6},{5,7},{6,4},{7,5},{8,10},{9,11},{10,... | collective-permute-start | bytes 196616 | tf_op jit(solution)/shard_map/ppermute | solution.py:308
  32.3 7.0 %collective-permute-start.4 = (f32[128,128]{1,0:T(8,128)S(1)}, f32[128,128]{1,0:T(8,128)S(1)}, u32[]{:S(2)}, u32[]{:S(2)}) collective-permute-start(f32[128,128]{1,0:T(8,128)S(1)} %get-tuple-element.41), channel_id=1, source_target_pairs={{0,1},{1,2},{2,3},{3,0},{4,5},{5,6},{6,7},{7,4},{8,9},{9,10},{10,1... | collective-permute-start | bytes 196616 | tf_op jit(solution)/shard_map/ppermute | solution.py:308
  32.4 8.7 %collective-permute-start.5 = (f32[128,128]{1,0:T(8,128)S(1)}, f32[128,128]{1,0:T(8,128)S(1)}, u32[]{:S(2)}, u32[]{:S(2)}) collective-permute-start(f32[128,128]{1,0:T(8,128)S(1)} %get-tuple-element.42), channel_id=1, source_target_pairs={{0,2},{1,3},{2,0},{3,1},{4,6},{5,7},{6,4},{7,5},{8,10},{9,11},{10,... | collective-permute-start | bytes 196616 | tf_op jit(solution)/shard_map/ppermute | solution.py:308
  33.7 7.4 %collective-permute-start.6 = (f32[128,128]{1,0:T(8,128)S(1)}, f32[128,128]{1,0:T(8,128)S(1)}, u32[]{:S(2)}, u32[]{:S(2)}) collective-permute-start(f32[128,128]{1,0:T(8,128)S(1)} %get-tuple-element.43), channel_id=1, source_target_pairs={{0,3},{1,0},{2,1},{3,2},{4,7},{5,4},{6,5},{7,6},{8,11},{9,8},{10,9... | collective-permute-start | bytes 196616 | tf_op jit(solution)/shard_map/ppermute | solution.py:308
  41.9 4.6 %collective-permute-start.7 = (f32[128,128]{1,0:T(8,128)S(1)}, f32[128,128]{1,0:T(8,128)S(1)}, u32[]{:S(2)}, u32[]{:S(2)}) collective-permute-start(f32[128,128]{1,0:T(8,128)S(1)} %get-tuple-element.45.right), channel_id=1, source_target_pairs={{0,4},{4,8},{8,12},{12,16},{16,20},{20,24},{24,28},{28,0},{1,5},{5... | collective-permute-start | bytes 196616 | tf_op jit(solution)/shard_map/ppermute | solution.py:308
  42.0 4.6 %collective-permute-start.8 = (f32[128,128]{1,0:T(8,128)S(1)}, f32[128,128]{1,0:T(8,128)S(1)}, u32[]{:S(2)}, u32[]{:S(2)}) collective-permute-start(f32[128,128]{1,0:T(8,128)S(1)} %get-tuple-element.44.left), channel_id=1, source_target_pairs={{0,28},{4,0},{8,4},{12,8},{16,12},{20,16},{24,20},{28,24},{1,29},{... | collective-permute-start | bytes 196616 | tf_op jit(solution)/shard_map/ppermute | solution.py:308
  47.3 7.3 %collective-permute-start.10 = (f32[128,128]{1,0:T(8,128)S(1)}, f32[128,128]{1,0:T(8,128)S(1)}, u32[]{:S(2)}, u32[]{:S(2)}) collective-permute-start(f32[128,128]{1,0:T(8,128)S(1)} %get-tuple-element.47.refs_0_), channel_id=1, source_target_pairs={{0,2},{1,3},{2,0},{3,1},{4,6},{5,7},{6,4},{7,5},{8,10},{9,11},{10,... | collective-permute-start | bytes 196616 | tf_op jit(solution)/shard_map/ppermute | solution.py:308
  47.9 6.7 %collective-permute-start.11 = (f32[128,128]{1,0:T(8,128)S(1)}, f32[128,128]{1,0:T(8,128)S(1)}, u32[]{:S(2)}, u32[]{:S(2)}) collective-permute-start(f32[128,128]{1,0:T(8,128)S(1)} %get-tuple-element.48), channel_id=1, source_target_pairs={{0,3},{1,0},{2,1},{3,2},{4,7},{5,4},{6,5},{7,6},{8,11},{9,8},{10,9... | collective-permute-start | bytes 196616 | tf_op jit(solution)/shard_map/ppermute | solution.py:308
  51.3 6.1 %collective-permute-start.9 = (f32[128,128]{1,0:T(8,128)S(1)}, f32[128,128]{1,0:T(8,128)S(1)}, u32[]{:S(2)}, u32[]{:S(2)}) collective-permute-start(f32[128,128]{1,0:T(8,128)S(1)} %get-tuple-element.48), channel_id=1, source_target_pairs={{0,1},{1,2},{2,3},{3,0},{4,5},{5,6},{6,7},{7,4},{8,9},{9,10},{10,1... | collective-permute-start | bytes 196616 | tf_op jit(solution)/shard_map/ppermute | solution.py:308
  62.3 5.2 %collective-permute-start.12 = (f32[128,128]{1,0:T(8,128)S(1)}, f32[128,128]{1,0:T(8,128)S(1)}, u32[]{:S(2)}, u32[]{:S(2)}) collective-permute-start(f32[128,128]{1,0:T(8,128)S(1)} %get-tuple-element.49.refs_0_), channel_id=1, source_target_pairs={{0,2},{1,3},{2,0},{3,1},{4,6},{5,7},{6,4},{7,5},{8,10},{9,11},{10,... | collective-permute-start | bytes 196616 | tf_op jit(solution)/shard_map/ppermute | solution.py:308
  72.6 6.2 %collective-permute-start.13 = (f32[128,128]{1,0:T(8,128)S(1)}, f32[128,128]{1,0:T(8,128)S(1)}, u32[]{:S(2)}, u32[]{:S(2)}) collective-permute-start(f32[128,128]{1,0:T(8,128)S(1)} %get-tuple-element.56), channel_id=1, source_target_pairs={{0,1},{1,2},{2,3},{3,0},{4,5},{5,6},{6,7},{7,4},{8,9},{9,10},{10,1... | collective-permute-start | bytes 196616 | tf_op jit(solution)/shard_map/ppermute | solution.py:308
  72.7 7.3 %collective-permute-start.14 = (f32[128,128]{1,0:T(8,128)S(1)}, f32[128,128]{1,0:T(8,128)S(1)}, u32[]{:S(2)}, u32[]{:S(2)}) collective-permute-start(f32[128,128]{1,0:T(8,128)S(1)} %get-tuple-element.57), channel_id=1, source_target_pairs={{0,2},{1,3},{2,0},{3,1},{4,6},{5,7},{6,4},{7,5},{8,10},{9,11},{10,... | collective-permute-start | bytes 196616 | tf_op jit(solution)/shard_map/ppermute | solution.py:308
  75.6 4.8 %collective-permute-start.15 = (f32[128,128]{1,0:T(8,128)S(1)}, f32[128,128]{1,0:T(8,128)S(1)}, u32[]{:S(2)}, u32[]{:S(2)}) collective-permute-start(f32[128,128]{1,0:T(8,128)S(1)} %get-tuple-element.58), channel_id=1, source_target_pairs={{0,3},{1,0},{2,1},{3,2},{4,7},{5,4},{6,5},{7,6},{8,11},{9,8},{10,9... | collective-permute-start | bytes 196616 | tf_op jit(solution)/shard_map/ppermute | solution.py:308
  81.1 4.7 %collective-permute-start.16 = (f32[128,128]{1,0:T(8,128)S(1)}, f32[128,128]{1,0:T(8,128)S(1)}, u32[]{:S(2)}, u32[]{:S(2)}) collective-permute-start(f32[128,128]{1,0:T(8,128)S(1)} %get-tuple-element.60.right), channel_id=1, source_target_pairs={{0,4},{4,8},{8,12},{12,16},{16,20},{20,24},{24,28},{28,0},{1,5},{5... | collective-permute-start | bytes 196616 | tf_op jit(solution)/shard_map/ppermute | solution.py:308
  81.2 4.7 %collective-permute-start.17 = (f32[128,128]{1,0:T(8,128)S(1)}, f32[128,128]{1,0:T(8,128)S(1)}, u32[]{:S(2)}, u32[]{:S(2)}) collective-permute-start(f32[128,128]{1,0:T(8,128)S(1)} %get-tuple-element.59.left), channel_id=1, source_target_pairs={{0,28},{4,0},{8,4},{12,8},{16,12},{20,16},{24,20},{28,24},{1,29},{... | collective-permute-start | bytes 196616 | tf_op jit(solution)/shard_map/ppermute | solution.py:308
  83.8 6.4 %collective-permute-start.21 = (f32[128,128]{1,0:T(8,128)S(1)}, f32[128,128]{1,0:T(8,128)S(1)}, u32[]{:S(2)}, u32[]{:S(2)}) collective-permute-start(f32[128,128]{1,0:T(8,128)S(1)} %get-tuple-element.62.refs_0_), channel_id=1, source_target_pairs={{0,1},{1,0},{2,3},{3,2},{4,5},{5,4},{6,7},{7,6},{8,9},{9,8},{10,11... | collective-permute-start | bytes 196616 | tf_op jit(solution)/shard_map/ppermute | solution.py:320
  85.1 5.1 %collective-permute-start.22 = (f32[128,128]{1,0:T(8,128)S(1)}, f32[128,128]{1,0:T(8,128)S(1)}, u32[]{:S(2)}, u32[]{:S(2)}) collective-permute-start(f32[128,128]{1,0:T(8,128)S(1)} %get-tuple-element.63.refs_2_), channel_id=1, source_target_pairs={{0,1},{1,0},{2,3},{3,2},{4,5},{5,4},{6,7},{7,6},{8,9},{9,8},{10,11... | collective-permute-start | bytes 196616 | tf_op jit(solution)/shard_map/ppermute | solution.py:320
  86.0 6.7 %collective-permute-start.18 = (f32[128,128]{1,0:T(8,128)S(1)}, f32[128,128]{1,0:T(8,128)S(1)}, u32[]{:S(2)}, u32[]{:S(2)}) collective-permute-start(f32[128,128]{1,0:T(8,128)S(1)} %shard_map.85.refs_0_), channel_id=1, source_target_pairs={{0,1},{1,2},{2,3},{3,0},{4,5},{5,6},{6,7},{7,4},{8,9},{9,10},{10,1... | collective-permute-start | bytes 196616 | tf_op jit(solution)/shard_map/ppermute | solution.py:308
  87.3 8.3 %collective-permute-start.19 = (f32[128,128]{1,0:T(8,128)S(1)}, f32[128,128]{1,0:T(8,128)S(1)}, u32[]{:S(2)}, u32[]{:S(2)}) collective-permute-start(f32[128,128]{1,0:T(8,128)S(1)} %shard_map.85.refs_0_), channel_id=1, source_target_pairs={{0,2},{1,3},{2,0},{3,1},{4,6},{5,7},{6,4},{7,5},{8,10},{9,11},{10,... | collective-permute-start | bytes 196616 | tf_op jit(solution)/shard_map/ppermute | solution.py:308
  89.3 6.3 %collective-permute-start.20 = (f32[128,128]{1,0:T(8,128)S(1)}, f32[128,128]{1,0:T(8,128)S(1)}, u32[]{:S(2)}, u32[]{:S(2)}) collective-permute-start(f32[128,128]{1,0:T(8,128)S(1)} %shard_map.85.refs_0_), channel_id=1, source_target_pairs={{0,3},{1,0},{2,1},{3,2},{4,7},{5,4},{6,5},{7,6},{8,11},{9,8},{10,9... | collective-permute-start | bytes 196616 | tf_op jit(solution)/shard_map/ppermute | solution.py:308
where the time goes:
time: 96.6 us; the launch traced here: 96.3 us
  waiting for transfers between devices  33.5 us (35%)
  starting transfers between devices  32.6 us (34%)
  Pallas kernels  25.5 us (26%)
  local copies, waits for them, and re-layouts  3.94 us (4%)
    ppermute x20, waiting for transfers between devices, shift(): return lax.ppermute(value, axis, ring(axis, steps))  33.5 us
    ppermute x20, starting transfers between devices, shift(): return lax.ppermute(value, axis, ring(axis, steps))  27.4 us
    pallas_call x11, Pallas kernels, call(): pl.pallas_call(body, out_shape=[jax.ShapeDtypeStruct(s, f32) for s in out...  25.5 us
    ppermute x3, starting transfers between devices, within(): return lax.ppermute(value, axis, pairs)  5.14 us
    unnamed x12, local copies, waits for them, and re-layouts  3.71 us
  transfers between devices with their start and end apart: 23, of which 14 were waited for; matrix products, arithmetic and copies ran while one was open for 2% of the time, Pallas kernels for 5%

commit v1 on v0

v1 whole, which is shorter than its diff:
```python
import math

import jax
import jax.numpy as jnp
import numpy as np
from jax import lax
from jax.experimental import pallas as pl
from jax.experimental.pallas import tpu as pltpu
from jax.sharding import PartitionSpec as P

HALO = 64
STEPS = 2
TILE_COLS = 8
SUB = 8
CHAIN = 2

learning_rate = 0.5

f32 = jnp.float32
bf16 = jnp.bfloat16

VMEM = pl.BlockSpec(memory_space=pltpu.VMEM)
SMEM = pl.BlockSpec(memory_space=pltpu.SMEM)


def dft_matrix(order):
    index = np.arange(order)
    angle = (np.outer(index, index) % order) * (2.0 * math.pi / order)
    factor = 1.0 / math.sqrt(order)
    cos, sin = np.cos(angle) * factor, -np.sin(angle) * factor
    table = np.block([[cos, sin], [-sin, cos]])
    high = table.astype(bf16)
    low = (table - high.astype(np.float64)).astype(bf16)
    return np.stack([high, low])


def call(body, outs, args, scratch=(), aliases=None, mib=24):
    specs = [SMEM if a.shape == (1,) else VMEM for a in args]
    return pl.pallas_call(
        body,
        out_shape=[jax.ShapeDtypeStruct(s, f32) for s in outs],
        in_specs=specs,
        out_specs=[VMEM] * len(outs),
        scratch_shapes=list(scratch),
        input_output_aliases=aliases or {},
        compiler_params=pltpu.CompilerParams(vmem_limit_bytes=mib << 20),
    )(*args)


def halves(x):
    high = x.astype(bf16)
    return high, (x - high.astype(f32)).astype(bf16)


def product(x, high, low):
    xh, xl = halves(x)
    dot = lambda a, b: jnp.dot(a, b, preferred_element_type=f32)
    return dot(xh, high) + dot(xl, high) + dot(xh, low)


def flip(x, k):
    rows = []
    for i in range(x.shape[0] // k):
        part = x[i * k : (i + 1) * k]
        rows.append(jnp.concatenate([part[:, :k].T, part[:, k:].T], axis=1))
    return jnp.concatenate(rows, axis=0)


def dft(waves, high, low):
    k = waves[0].shape[0]
    chains = [jnp.concatenate(waves[i : i + CHAIN], axis=0) for i in range(0, len(waves), CHAIN)]
    chains = [product(x, high, low) for x in chains]
    chains = [flip(x, k) for x in chains]
    chains = [product(x, high, low) for x in chains]
    return [y[i : i + k] for y in chains for i in range(0, y.shape[0], k)]


def pair(re, im):
    return jnp.concatenate([re, im], axis=1)


def window(plane, row, col, k):
    tall, width = k + SUB, plane.shape[1]
    base = pl.multiple_of(row - row % SUB, SUB)
    part = pltpu.roll(plane[pl.ds(base, tall), :], (width - col) % width, 1)[:, :k]
    return pltpu.roll(part, (tall - row % SUB) % tall, 0)[:k]


def add_window(ext, value, row, col):
    k, width = value.shape[0], ext.shape[1]
    wide = pltpu.roll(pair(value, jnp.zeros((k, width - k), f32)), col, 1)
    tall = jnp.concatenate([wide, jnp.zeros((SUB, width), f32)], axis=0)
    where = pl.ds(pl.multiple_of(row - row % SUB, SUB), k + SUB)
    ext[where, :] = ext[where, :] + pltpu.roll(tall, row % SUB, 0)


def spot(pos, which):
    value = pos[...].astype(f32)
    mine = lax.broadcasted_iota(jnp.int32, value.shape, 0) == which
    first = lax.broadcasted_iota(jnp.int32, value.shape, 1) == 0
    row = jnp.sum(jnp.where(mine & first, value, 0.0)).astype(jnp.int32)
    col = jnp.sum(jnp.where(mine & ~first, value, 0.0)).astype(jnp.int32)
    return row, col


def forward_modes(win, probes, cos_t, sin_t, table, u_out, psi_out, first, last):
    k = win.shape[1]
    high, low = table[0], table[1]
    cos, sin = cos_t[...], sin_t[...]
    ar, ai, br, bi = 1.0 + win[0], win[1], 1.0 + win[2], win[3]
    waves = []
    for m in range(first, last):
        pr, pi = probes[m, 0], probes[m, 1]
        waves.append(pair(ar * pr - ai * pi, ar * pi + ai * pr))
    turned = []
    for s in dft(waves, high, low):
        sr, si = s[:, :k], s[:, k:]
        turned.append(pair(cos * sr - sin * si, -(cos * si + sin * sr)))
    waves = []
    for m, u in enumerate(dft(turned, high, low), first):
        u_out[m] = u
        ur, ui = u[:, :k], u[:, k:]
        waves.append(pair(br * ur + bi * ui, bi * ur - br * ui))
    total = jnp.zeros((k, k), f32)
    for m, psi in enumerate(dft(waves, high, low), first):
        psi_out[m] = psi
        square = psi * psi
        total = total + (square[:, :k] + square[:, k:])
    return total.T


def pack(tile, to_left, to_right, copy):
    core = tile.shape[1]
    for p in range(0, tile.shape[0], 2):
        to_left[p // 2] = pair(tile[p][:, :HALO], tile[p + 1][:, :HALO])
        to_right[p // 2] = pair(tile[p][:, core - HALO :], tile[p + 1][:, core - HALO :])
    copy[...] = tile[...]


def hold(probe, probes):
    probes[0 : probe.shape[0]] = probe[...]


def first_forward(step_rows, rows):
    def body(index, pos, *refs):
        z = index[0]
        if rows:
            ext_ref, probes, cos_t, sin_t, table = refs[:5]
            win, owned, part, u_out, psi_out, ext = refs[5:]
            ext[...] = ext_ref[...]
        else:
            tile, from_left, from_right, probes, cos_t, sin_t, table = refs[:7]
            win, owned, part, u_out, psi_out, ext = refs[7:]
            planes, core = tile.shape[0], tile.shape[1]
            ext[...] = jnp.zeros(ext.shape, f32)
            for p in range(planes):
                at = slice(p % 2 * HALO, (p % 2 + 1) * HALO)
                ext[p, HALO : HALO + core, :] = jnp.concatenate(
                    [from_left[p // 2][:, at], tile[p], from_right[p // 2][:, at]], axis=1
                )
        planes, k = win.shape[0], win.shape[1]
        q = z % step_rows
        row, col = spot(pos, q)
        for p in range(planes):
            win[p] = window(ext.at[p], row, col, k)
        owned[...] = ext[z]
        half = probes.shape[0] // step_rows
        part[...] = forward_modes(win, probes, cos_t, sin_t, table, u_out, psi_out, 0, half)

    return body


def more_forward(win, probe, cos_t, sin_t, table, before, p_in, u_in, psi_in, part, probes, u_out, psi_out):
    first, last = probes.shape[0] - probe.shape[0], probes.shape[0]
    probes[first:last] = probe[...]
    part[...] = before[...] + forward_modes(
        win, probes, cos_t, sin_t, table, u_out, psi_out, first, last
    )


def next_forward(count):
    def body(index, *refs):
        pieces, refs = refs[:count], refs[count:]
        probes, cos_t, sin_t, table, win, part, u_out, psi_out = refs
        z = index[0]
        for j, piece in enumerate(pieces):
            win[z ^ j] = piece[...]
        part[...] = forward_modes(
            win, probes, cos_t, sin_t, table, u_out, psi_out, 0, probes.shape[0]
        )

    return body


def backward(step, step_rows, parts, count):
    def body(index, *refs):
        partials, refs = refs[:parts], refs[parts:]
        measured, win, probes, u_in, psi_in, cos_t, sin_t, table = refs[:8]
        sends, grads = refs[8 : 8 + count], refs[8 + count]
        z = index[0]
        k = win.shape[1]
        high, low = table[0], table[1]
        cos, sin = cos_t[...], sin_t[...]
        total = partials[0][...]
        for extra in partials[1:]:
            total = total + extra[...]
        sends[1][1] = total
        twice = (2.0 * (total - measured[step * step_rows + z % step_rows])).T
        br, bi = 1.0 + win[2], win[3]
        zero = jnp.zeros((k, k), f32)
        waves = []
        for m in range(probes.shape[0]):
            psi = psi_in[m]
            waves.append(pair(twice * psi[:, :k], -(twice * psi[:, k:])))
        turned = []
        sum_r, sum_i = zero, zero
        for m, g in enumerate(dft(waves, high, low)):
            gr, gi = g[:, :k], -g[:, k:]
            u = u_in[m]
            ur, ui = u[:, :k], u[:, k:]
            sum_r = sum_r + (ur * gr - ui * gi)
            sum_i = sum_i + (ur * gi + ui * gr)
            turned.append(pair(br * gr + bi * gi, br * gi - bi * gr))
        grads[2], grads[3] = sum_r, sum_i
        waves = []
        for s in dft(turned, high, low):
            sr, si = s[:, :k], s[:, k:]
            waves.append(pair(cos * sr + sin * si, sin * sr - cos * si))
        sum_r, sum_i = zero, zero
        for m, g in enumerate(dft(waves, high, low)):
            gr, gi = g[:, :k], -g[:, k:]
            pr, pi = probes[m, 0], probes[m, 1]
            sum_r = sum_r + (pr * gr + pi * gi)
            sum_i = sum_i + (pr * gi - pi * gr)
        grads[0], grads[1] = sum_r, sum_i
        for j in range(count):
            if j == 1:
                sends[j][0] = grads[z ^ j]
            else:
                sends[j][...] = grads[z ^ j]

    return body


def scatter(step, step_rows, count, rows):
    def body(index, pos, *refs):
        pieces, outs, ext = refs[:count], refs[count:-1], refs[-1]
        z = index[0]
        q = z % step_rows
        width = ext.shape[1]
        ext[...] = jnp.zeros(ext.shape, f32)
        values = [piece[0] if j == 1 else piece[...] for j, piece in enumerate(pieces)]
        for i in range(step_rows):
            total = values[i]
            for j in range(i + step_rows, count, step_rows):
                total = total + values[j]
            which = step * step_rows + (q ^ i)
            add_window(ext, total, *spot(pos, which))
        if rows:
            outs[0][...] = ext[...]
        else:
            half = width // 2
            core = outs[0].shape[0]
            middle = ext[HALO : HALO + core, :]
            outs[0][...], outs[1][...] = middle[:, :half], middle[:, half:]

    return body


def updated_rows(left, right, from_left, from_right, owned):
    grad = pair(left[...] + from_left[...], right[...] + from_right[...])
    return owned[HALO : HALO + grad.shape[0], :] - learning_rate * grad


def next_windows(step, step_rows, source, z, pos, outs):
    q = z % step_rows
    k = outs[0].shape[0]
    for i, out in enumerate(outs):
        which = step * step_rows + (q ^ i)
        out[...] = window(source, *spot(pos, which), k)


def update(step, step_rows):
    def body(index, pos, left, right, from_left, from_right, owned, fresh, *outs):
        z = index[0]
        fresh[...] = jnp.zeros(fresh.shape, f32)
        fresh[HALO : HALO + left.shape[0], :] = updated_rows(left, right, from_left, from_right, owned)
        next_windows(step, step_rows, fresh, z, pos, outs)

    return body


def update_middle(left, right, from_left, from_right, owned, middle):
    middle[...] = updated_rows(left, right, from_left, from_right, owned)


def only_windows(step, step_rows):
    def body(index, pos, owned, *outs):
        next_windows(step, step_rows, owned, index[0], pos, outs)

    return body


def last_update(left, right, from_left, from_right, owned, core):
    middle = updated_rows(left, right, from_left, from_right, owned)
    core[...] = middle[:, HALO : middle.shape[1] - HALO]


def gather_planes(count):
    def body(index, *refs):
        out = refs[count]
        for j in range(count):
            out[index[0] ^ j] = refs[j][...]

    return body


def gather_intensities(step_rows):
    def body(index, *refs):
        out = refs[-1]
        q = index[0] % step_rows
        for i, ref in enumerate(refs[:-1]):
            step, j = divmod(i, step_rows)
            out[step * step_rows + (q ^ j)] = ref[1]

    return body


def across(value, axis, bits):
    return lax.ppermute(value, axis, [(i, i ^ bits) for i in range(lax.axis_size(axis))])


def around(value, steps):
    count = lax.axis_size("tile")
    return lax.ppermute(value, "tile", [(i, (i + steps) % count) for i in range(count)])


def from_behind(value, axis, steps):
    count = lax.axis_size(axis)
    first, last = (max(0, -steps), min(count, count - steps))
    return lax.ppermute(value, axis, [(source, source + steps) for source in range(first, last)])


def local(object_tiles, probe, propagator_phase, measured, positions):
    layers, core = object_tiles.shape[1], object_tiles.shape[3]
    count = layers * 2
    k = probe.shape[-1]
    step_rows = positions.shape[0] // STEPS
    modes = probe.shape[0] * step_rows
    group, tiles = lax.axis_size("mode"), lax.axis_size("tile")
    assert layers == 2 and count == group and step_rows == 2 and core == 2 * HALO
    rows = tiles > TILE_COLS
    extent = core + 2 * HALO
    tall = (extent + SUB, extent)
    index = lax.axis_index("mode").astype(jnp.int32).reshape(1)
    planes = object_tiles.reshape(count, core, core)
    flat, wave, held = (k, k), (modes, k, 2 * k), (modes,) + probe.shape[1:]

    other_probe = across(probe, "mode", 1)
    packed = (count // 2, core, 2 * HALO)
    to_left, to_right, planes = call(pack, [packed, packed, planes.shape], (planes,))
    from_right, from_left = around(to_left, -1), around(to_right, 1)
    cos_t, sin_t = jnp.cos(propagator_phase.T), jnp.sin(propagator_phase.T)
    optics = (cos_t, sin_t, jnp.asarray(dft_matrix(k)))
    (probes,) = call(hold, [held], (probe,))

    if rows:

        def unpacked(value):
            return value.reshape(-1, core, 2, HALO).transpose(0, 2, 1, 3).reshape(count, core, HALO)

        wide = jnp.concatenate([unpacked(from_left), planes, unpacked(from_right)], axis=2)
        above = from_behind(wide[:, core - HALO :], "tile", TILE_COLS)
        below = from_behind(wide[:, :HALO], "tile", -TILE_COLS)
        slack = jnp.zeros((count, SUB, extent), f32)
        objects = (jnp.concatenate([above, wide, below, slack], axis=1),)
    else:
        objects = (planes, from_left, from_right)

    win, owned, part, u, psi = call(
        first_forward(step_rows, rows),
        [(count, k, k), tall, flat, wave, wave],
        (index, positions) + objects + (probes,) + optics,
        [pltpu.VMEM((count,) + tall, f32)],
    )
    part, probes, u, psi = call(
        more_forward,
        [flat, held, wave, wave],
        (win, other_probe) + optics + (part, probes, u, psi),
        aliases={6: 1, 7: 2, 8: 3},
    )

    kept = []
    for step in range(STEPS):
        partials = [part] + [across(part, "mode", j) for j in range(step_rows, group, step_rows)]
        sends = call(
            backward(step, step_rows, len(partials), count),
            [flat, (2,) + flat] + [flat] * (count - 2),
            (index,) + tuple(partials) + (measured, win, probes, u, psi) + optics,
            [pltpu.VMEM((count, k, k), f32)],
        )
        pieces = [sends[0]] + [across(sends[j], "mode", j) for j in range(1, group)]
        kept += [sends[1], pieces[1]]
        half = (core, extent // 2)
        grads = call(
            scatter(step, step_rows, count, rows),
            [tall] if rows else [half, half],
            (index, positions) + tuple(pieces),
            [pltpu.VMEM(tall, f32)],
        )
        if rows:
            whole = grads[0]
            middle = whole[HALO : HALO + core]
            middle = middle.at[core - HALO :].add(from_behind(whole[:HALO], "tile", -TILE_COLS))
            middle = middle.at[:HALO].add(from_behind(whole[HALO + core : extent], "tile", TILE_COLS))
            grads = (middle[:, : extent // 2], middle[:, extent // 2 :])
        left, right = grads
        sums = (left, right, around(right, 1), around(left, -1), owned)
        if step + 1 == STEPS:
            break
        if rows:
            (middle,) = call(update_middle, [(core, extent)], sums)
            above = from_behind(middle[core - HALO :], "tile", TILE_COLS)
            below = from_behind(middle[:HALO], "tile", -TILE_COLS)
            slack = jnp.zeros((SUB, extent), f32)
            owned = jnp.concatenate([above, middle, below, slack], axis=0)
            outs = call(only_windows(step + 1, step_rows), [flat] * step_rows, (index, positions, owned))
        else:
            out = call(
                update(step + 1, step_rows),
                [tall] + [flat] * step_rows,
                (index, positions) + sums,
            )
            owned, outs = out[0], out[1:]
        pieces = [outs[0]] + [across(outs[j % step_rows], "mode", j) for j in range(1, group)]
        win, part, u, psi = call(
            next_forward(count),
            [(count, k, k), flat, wave, wave],
            (index,) + tuple(pieces) + (probes,) + optics,
        )

    (plane,) = call(last_update, [(core, core)], sums)
    pieces = [plane] + [across(plane, "mode", j) for j in range(1, group)]
    (updated,) = call(gather_planes(count), [(count, core, core)], (index,) + tuple(pieces))
    (intensities,) = call(gather_intensities(step_rows), [measured.shape], (index,) + tuple(kept))
    return (updated.reshape(object_tiles.shape), intensities)


def solution(mesh):
    return jax.shard_map(
        local,
        mesh=mesh,
        in_specs=(
            P("tile", None, None, None, None),
            P("mode", None, None, None),
            P(),
            P("tile", None, None),
            P("tile", None),
        ),
        out_specs=(P("tile", None, None, None, None), P("tile", None, None)),
        check_vma=False,
    )
```

time: 96.6 us -> 83.8 us (0.87)
  Pallas kernels: 25.5 us -> 15.9 us
  starting transfers between devices: 32.6 us -> 28.1 us
  waiting for transfers between devices: 33.5 us -> 35.7 us
    pallas_call x11 -> x13, Pallas kernels: 25.5 us -> 15.9 us  [call(): pl.pallas_call(body, out_shape=[jax.ShapeDtypeStruct(s, f32) for s in out...]
    ppermute x23 -> x21, starting transfers between devices: 32.6 us -> 28.1 us  [the longest x15 24.3 us: across(): lax.ppermute(value, axis, [(i, i ^ bits) for i in range(lax.axis_size(axi...]
    ppermute x23 -> x21, waiting for transfers between devices: 33.5 us -> 35.7 us  [the longest x15 26.2 us: across(): lax.ppermute(value, axis, [(i, i ^ bits) for i in range(lax.axis_size(axi...]
    unnamed x12 -> x14, local copies, waits for them, and re-layouts: 3.71 us -> 2.89 us
  transfers between devices with their start and end apart: 23 -> 21, of which waited for: 14 -> 17; matrix products, arithmetic and copies ran while one was open for 2% -> 1% of each run, Pallas kernels for 5% -> 4%
where the time goes in v1:
time: 83.8 us; the launch traced here: 83.6 us
  waiting for transfers between devices  35.7 us (43%)
  starting transfers between devices  28.1 us (34%)
  Pallas kernels  15.9 us (19%)
  local copies, waits for them, and re-layouts  3.13 us (4%)
    ppermute x15, waiting for transfers between devices, across(): lax.ppermute(value, axis, [(i, i ^ bits) for i in range(lax.axis_size(axi...  26.2 us
    ppermute x15, starting transfers between devices, across(): lax.ppermute(value, axis, [(i, i ^ bits) for i in range(lax.axis_size(axi...  24.3 us
    pallas_call x13, Pallas kernels, call(): pl.pallas_call(body, out_shape=[jax.ShapeDtypeStruct(s, f32) for s in out...  15.9 us
    ppermute x6, waiting for transfers between devices, around(): lax.ppermute(value, 'tile', [(i, (i + steps) % count) for i in range(coun...  9.44 us
    ppermute x6, starting transfers between devices, around(): lax.ppermute(value, 'tile', [(i, (i + steps) % count) for i in range(coun...  3.8 us
    unnamed x14, local copies, waits for them, and re-layouts  2.89 us
  transfers between devices with their start and end apart: 21, of which 17 were waited for; matrix products, arithmetic and copies ran while one was open for 1% of the time, Pallas kernels for 4%

profile of v1, /device:TPU:0, one launch (start us, length us, event | category | flops | bytes accessed | tf_op | source)
XLA Modules:
  0.0 83.6 jit_solution(11658729911746029078)
XLA Ops:
  0.6 3.1 %collective-permute-start.2 = (f32[4,2,128,128]{3,2,1,0:T(8,128)}, f32[4,2,128,128]{3,2,1,0:T(8,128)S(1)}, u32[]{:S(2)}, u32[]{:S(2)}) collective-permute-start(f32[4,2,128,128]{3,2,1,0:T(8,128)} %probe.1), channel_id=1, source_target_pairs={{0,1},{1,0},{2,3},{3,2},{4,5},{5,4},{6,7},{7,6},{8,9},{9,8},{10,11... | collective-permute-start | bytes 1572872 | tf_op jit(solution)/shard_map/ppermute | solution.py:330
  3.7 0.9 %copy-done.3 = f32[1,2,2,128,128]{4,3,2,1,0:T(8,128)S(1)} copy-done((f32[1,2,2,128,128]{4,3,2,1,0:T(8,128)S(1)}, f32[1,2,2,128,128]{4,3,2,1,0:T(8,128)}, u32[]{:S(2)}) %copy-start.3) | copy-done | bytes 262168
  4.7 0.1 shard_map.77
  4.8 0.1 collective-permute-start
  4.9 2.6 %collective-permute-start.1 = (f32[2,128,128]{2,1,0:T(8,128)S(1)}, f32[2,128,128]{2,1,0:T(8,128)S(1)}, u32[]{:S(2)}, u32[]{:S(2)}) collective-permute-start(f32[2,128,128]{2,1,0:T(8,128)S(1)} %get-tuple-element.35), channel_id=1, source_target_pairs={{0,28},{4,0},{8,4},{12,8},{16,12},{20,16},{24,20},{28,24},{1,29},{... | collective-permute-start | bytes 393224 | tf_op jit(solution)/shard_map/ppermute | solution.py:335
  7.5 1.0 %copy-done.2 = f32[4,2,128,128]{3,2,1,0:T(8,128)S(1)} copy-done((f32[4,2,128,128]{3,2,1,0:T(8,128)S(1)}, f32[4,2,128,128]{3,2,1,0:T(8,128)}, u32[]{:S(2)}) %copy-start.2) | copy-done | bytes 524312
  8.6 0.0 copy-start
  8.6 0.6 copy-done.5
  9.3 0.1 copy.16.pos
  9.3 0.1 copy-done.4
  9.4 0.1 copy.11
  9.5 0.2 sine_bitcast_fusion
  9.8 0.4 collective-permute-done.refs_1_
  10.2 0.0 collective-permute-done.1.refs_2_
  10.2 0.0 copy-done
  10.2 2.6 %shard_map.79 = (f32[4,128,128]{2,1,0:T(8,128)S(1)}, f32[264,256]{1,0:T(8,128)S(1)}, f32[128,128]{1,0:T(8,128)S(1)}, f32[8,128,256]{2,1,0:T(8,128)S(1)}, f32[8,128,256]{2,1,0:T(8,128)S(1)}) custom-call(s32[1]{0:T(128)} %bitcast.index, s32[4,2]{1,0:T(4,128)S(1)} %copy.16.pos, f32[4,128,128]{2,1,0:T(8,128)S(1)} %get-tuple-element.33.refs_0_, ...), custom_call_target="tpu_custom_call" | custom-call | tf_op jit(solution)/shard_map/pallas_call | solution.py:39
  12.8 3.1 %collective-permute-done.2.probe = f32[4,2,128,128]{3,2,1,0:T(8,128)S(1)} collective-permute-done((f32[4,2,128,128]{3,2,1,0:T(8,128)}, f32[4,2,128,128]{3,2,1,0:T(8,128)S(1)}, u32[]{:S(2)}, u32[]{:S(2)}) %collective-permute-start.2) | collective-permute-done | bytes 524320 | tf_op jit(solution)/shard_map/ppermute | solution.py:330
  15.9 2.2 %shard_map.80 = (f32[128,128]{1,0:T(8,128)S(1)}, f32[8,2,128,128]{3,2,1,0:T(8,128)S(1)}, f32[8,128,256]{2,1,0:T(8,128)S(1)}, f32[8,128,256]{2,1,0:T(8,128)S(1)}) custom-call(f32[4,128,128]{2,1,0:T(8,128)S(1)} %get-tuple-element.36.win.refs_3_, ...), custom_call_target="tpu_custom_call", output_to_operand_aliasing={{1}: (6, {}), {2}: (7, {}), {3}: (8, {})} | custom-call | tf_op jit(solution)/shard_map/pallas_call | solution.py:39
  18.1 2.8 %collective-permute-start.3 = (f32[128,128]{1,0:T(8,128)S(1)}, f32[128,128]{1,0:T(8,128)S(1)}, u32[]{:S(2)}, u32[]{:S(2)}) collective-permute-start(f32[128,128]{1,0:T(8,128)S(1)} %get-tuple-element.40.refs_0_), channel_id=1, source_target_pairs={{0,2},{1,3},{2,0},{3,1},{4,6},{5,7},{6,4},{7,5},{8,10},{9,11},{10,... | collective-permute-start | bytes 196616 | tf_op jit(solution)/shard_map/ppermute | solution.py:330
  20.9 2.4 %collective-permute-done.3.refs_1_ = f32[128,128]{1,0:T(8,128)S(1)} collective-permute-done((f32[128,128]{1,0:T(8,128)S(1)}, f32[128,128]{1,0:T(8,128)S(1)}, u32[]{:S(2)}, u32[]{:S(2)}) %collective-permute-start.3) | collective-permute-done | bytes 65568 | tf_op jit(solution)/shard_map/ppermute | solution.py:330
  23.3 0.0 copy-done.1
  23.3 2.8 %shard_map.81 = (f32[128,128]{1,0:T(8,128)S(1)}, f32[2,128,128]{2,1,0:T(8,128)S(1)}, f32[128,128]{1,0:T(8,128)S(1)}, f32[128,128]{1,0:T(8,128)S(1)}) custom-call(s32[1]{0:T(128)} %bitcast.index, f32[128,128]{1,0:T(8,128)S(1)} %get-tuple-element.40.refs_0_, f32[128,128]{1,0:T(8,128)S(1)} %collective-permute-done.3.refs_1_, f32[4,128,128]{2,1,0:T(8,128)S(1)} %copy-done.1, ...), custom_call_target="tpu_custom_call" | custom-call | tf_op jit(solution)/shard_map/pallas_call | solution.py:39
  26.1 1.8 %collective-permute-start.4 = (f32[2,128,128]{2,1,0:T(8,128)S(1)}, f32[2,128,128]{2,1,0:T(8,128)S(1)}, u32[]{:S(2)}, u32[]{:S(2)}) collective-permute-start(f32[2,128,128]{2,1,0:T(8,128)S(1)} %get-tuple-element.45.refs_0_), channel_id=1, source_target_pairs={{0,1},{1,0},{2,3},{3,2},{4,5},{5,4},{6,7},{7,6},{8,9},{9,8},{10,11... | collective-permute-start | bytes 393224 | tf_op jit(solution)/shard_map/ppermute | solution.py:330
  27.9 3.2 %collective-permute-start.5 = (f32[128,128]{1,0:T(8,128)S(1)}, f32[128,128]{1,0:T(8,128)S(1)}, u32[]{:S(2)}, u32[]{:S(2)}) collective-permute-start(f32[128,128]{1,0:T(8,128)S(1)} %get-tuple-element.46), channel_id=1, source_target_pairs={{0,2},{1,3},{2,0},{3,1},{4,6},{5,7},{6,4},{7,5},{8,10},{9,11},{10,... | collective-permute-start | bytes 196616 | tf_op jit(solution)/shard_map/ppermute | solution.py:330
  31.1 0.0 collective-permute-start.6
  31.1 2.8 %collective-permute-done.5.refs_2_ = f32[128,128]{1,0:T(8,128)S(1)} collective-permute-done((f32[128,128]{1,0:T(8,128)S(1)}, f32[128,128]{1,0:T(8,128)S(1)}, u32[]{:S(2)}, u32[]{:S(2)}) %collective-permute-start.5) | collective-permute-done | bytes 65568 | tf_op jit(solution)/shard_map/ppermute | solution.py:330
  33.9 3.2 %collective-permute-done.6.refs_3_ = f32[128,128]{1,0:T(8,128)S(1)} collective-permute-done((f32[128,128]{1,0:T(8,128)S(1)}, f32[128,128]{1,0:T(8,128)S(1)}, u32[]{:S(2)}, u32[]{:S(2)}) %collective-permute-start.6) | collective-permute-done | bytes 65568 | tf_op jit(solution)/shard_map/ppermute | solution.py:330
  37.2 0.0 collective-permute-done.4.refs_1_
  37.2 0.3 shard_map.82
  37.5 0.1 collective-permute-start.8
  37.6 0.5 collective-permute-start.7
  38.1 1.4 %collective-permute-done.8.from_right = f32[128,128]{1,0:T(8,128)S(1)} collective-permute-done((f32[128,128]{1,0:T(8,128)S(1)}, f32[128,128]{1,0:T(8,128)S(1)}, u32[]{:S(2)}, u32[]{:S(2)}) %collective-permute-start.8) | collective-permute-done | bytes 65568 | tf_op jit(solution)/shard_map/ppermute | solution.py:335
  39.5 3.5 %collective-permute-done.7.from_left = f32[128,128]{1,0:T(8,128)S(1)} collective-permute-done((f32[128,128]{1,0:T(8,128)S(1)}, f32[128,128]{1,0:T(8,128)S(1)}, u32[]{:S(2)}, u32[]{:S(2)}) %collective-permute-start.7) | collective-permute-done | bytes 65568 | tf_op jit(solution)/shard_map/ppermute | solution.py:335
  42.9 0.3 shard_map.83
  43.2 0.2 collective-permute-start.10
  43.4 1.3 %collective-permute-start.11 = (f32[128,128]{1,0:T(8,128)S(1)}, f32[128,128]{1,0:T(8,128)S(1)}, u32[]{:S(2)}, u32[]{:S(2)}) collective-permute-start(f32[128,128]{1,0:T(8,128)S(1)} %get-tuple-element.52), channel_id=1, source_target_pairs={{0,3},{1,2},{2,1},{3,0},{4,7},{5,6},{6,5},{7,4},{8,11},{9,10},{10,... | collective-permute-start | bytes 196616 | tf_op jit(solution)/shard_map/ppermute | solution.py:330
  44.6 2.1 %collective-permute-start.9 = (f32[128,128]{1,0:T(8,128)S(1)}, f32[128,128]{1,0:T(8,128)S(1)}, u32[]{:S(2)}, u32[]{:S(2)}) collective-permute-start(f32[128,128]{1,0:T(8,128)S(1)} %get-tuple-element.52), channel_id=1, source_target_pairs={{0,1},{1,0},{2,3},{3,2},{4,5},{5,4},{6,7},{7,6},{8,9},{9,8},{10,11... | collective-permute-start | bytes 196616 | tf_op jit(solution)/shard_map/ppermute | solution.py:330
  46.8 1.7 %collective-permute-done.10.refs_2_ = f32[128,128]{1,0:T(8,128)S(1)} collective-permute-done((f32[128,128]{1,0:T(8,128)S(1)}, f32[128,128]{1,0:T(8,128)S(1)}, u32[]{:S(2)}, u32[]{:S(2)}) %collective-permute-start.10) | collective-permute-done | bytes 65568 | tf_op jit(solution)/shard_map/ppermute | solution.py:330
  48.5 1.1 %collective-permute-done.11.refs_3_ = f32[128,128]{1,0:T(8,128)S(1)} collective-permute-done((f32[128,128]{1,0:T(8,128)S(1)}, f32[128,128]{1,0:T(8,128)S(1)}, u32[]{:S(2)}, u32[]{:S(2)}) %collective-permute-start.11) | collective-permute-done | bytes 65568 | tf_op jit(solution)/shard_map/ppermute | solution.py:330
  49.5 0.3 collective-permute-done.9.refs_1_
  49.9 2.8 %shard_map.84 = (f32[4,128,128]{2,1,0:T(8,128)S(1)}, f32[128,128]{1,0:T(8,128)S(1)}, f32[8,128,256]{2,1,0:T(8,128)S(1)}, f32[8,128,256]{2,1,0:T(8,128)S(1)}) custom-call(s32[1]{0:T(128)} %bitcast.index, f32[128,128]{1,0:T(8,128)S(1)} %get-tuple-element.51.refs_0_, f32[128,128]{1,0:T(8,128)S(1)} %collective-permute-done.9.refs_1_, ...), custom_call_target="tpu_custom_call" | custom-call | tf_op jit(solution)/shard_map/pallas_call | solution.py:39
  52.7 0.9 %collective-permute-start.12 = (f32[128,128]{1,0:T(8,128)S(1)}, f32[128,128]{1,0:T(8,128)S(1)}, u32[]{:S(2)}, u32[]{:S(2)}) collective-permute-start(f32[128,128]{1,0:T(8,128)S(1)} %get-tuple-element.53.refs_0_), channel_id=1, source_target_pairs={{0,2},{1,3},{2,0},{3,1},{4,6},{5,7},{6,4},{7,5},{8,10},{9,11},{10,... | collective-permute-start | bytes 196616 | tf_op jit(solution)/shard_map/ppermute | solution.py:330
  53.6 4.3 %collective-permute-done.12.refs_1_ = f32[128,128]{1,0:T(8,128)S(1)} collective-permute-done((f32[128,128]{1,0:T(8,128)S(1)}, f32[128,128]{1,0:T(8,128)S(1)}, u32[]{:S(2)}, u32[]{:S(2)}) %collective-permute-start.12) | collective-permute-done | bytes 65568 | tf_op jit(solution)/shard_map/ppermute | solution.py:330
  57.9 2.9 %shard_map.85 = (f32[128,128]{1,0:T(8,128)S(1)}, f32[2,128,128]{2,1,0:T(8,128)S(1)}, f32[128,128]{1,0:T(8,128)S(1)}, f32[128,128]{1,0:T(8,128)S(1)}) custom-call(s32[1]{0:T(128)} %bitcast.index, f32[128,128]{1,0:T(8,128)S(1)} %get-tuple-element.53.refs_0_, f32[128,128]{1,0:T(8,128)S(1)} %collective-permute-done.12.refs_1_, f32[4,128,128]{2,1,0:T(8,128)S(1)} %copy-done.1, ...), custom_call_target="tpu_custom_call" | custom-call | tf_op jit(solution)/shard_map/pallas_call | solution.py:39
  60.8 1.3 %collective-permute-start.13 = (f32[2,128,128]{2,1,0:T(8,128)S(1)}, f32[2,128,128]{2,1,0:T(8,128)S(1)}, u32[]{:S(2)}, u32[]{:S(2)}) collective-permute-start(f32[2,128,128]{2,1,0:T(8,128)S(1)} %get-tuple-element.58.refs_2_), channel_id=1, source_target_pairs={{0,1},{1,0},{2,3},{3,2},{4,5},{5,4},{6,7},{7,6},{8,9},{9,8},{10,11... | collective-permute-start | bytes 393224 | tf_op jit(solution)/shard_map/ppermute | solution.py:330
  62.1 1.7 %collective-permute-start.14 = (f32[128,128]{1,0:T(8,128)S(1)}, f32[128,128]{1,0:T(8,128)S(1)}, u32[]{:S(2)}, u32[]{:S(2)}) collective-permute-start(f32[128,128]{1,0:T(8,128)S(1)} %get-tuple-element.59), channel_id=1, source_target_pairs={{0,2},{1,3},{2,0},{3,1},{4,6},{5,7},{6,4},{7,5},{8,10},{9,11},{10,... | collective-permute-start | bytes 196616 | tf_op jit(solution)/shard_map/ppermute | solution.py:330
  63.8 1.5 %collective-permute-start.15 = (f32[128,128]{1,0:T(8,128)S(1)}, f32[128,128]{1,0:T(8,128)S(1)}, u32[]{:S(2)}, u32[]{:S(2)}) collective-permute-start(f32[128,128]{1,0:T(8,128)S(1)} %get-tuple-element.60), channel_id=1, source_target_pairs={{0,3},{1,2},{2,1},{3,0},{4,7},{5,6},{6,5},{7,4},{8,11},{9,10},{10,... | collective-permute-start | bytes 196616 | tf_op jit(solution)/shard_map/ppermute | solution.py:330
  65.2 2.7 %collective-permute-done.14.refs_2_ = f32[128,128]{1,0:T(8,128)S(1)} collective-permute-done((f32[128,128]{1,0:T(8,128)S(1)}, f32[128,128]{1,0:T(8,128)S(1)}, u32[]{:S(2)}, u32[]{:S(2)}) %collective-permute-start.14) | collective-permute-done | bytes 65568 | tf_op jit(solution)/shard_map/ppermute | solution.py:330
  68.0 1.9 %collective-permute-done.15.refs_3_ = f32[128,128]{1,0:T(8,128)S(1)} collective-permute-done((f32[128,128]{1,0:T(8,128)S(1)}, f32[128,128]{1,0:T(8,128)S(1)}, u32[]{:S(2)}, u32[]{:S(2)}) %collective-permute-start.15) | collective-permute-done | bytes 65568 | tf_op jit(solution)/shard_map/ppermute | solution.py:330
  69.9 0.0 collective-permute-done.13.refs_1_.refs_3_
  69.9 0.3 shard_map.86
  70.2 0.1 collective-permute-start.17
  70.3 0.5 collective-permute-start.16
  70.8 1.5 %collective-permute-done.17.from_right = f32[128,128]{1,0:T(8,128)S(1)} collective-permute-done((f32[128,128]{1,0:T(8,128)S(1)}, f32[128,128]{1,0:T(8,128)S(1)}, u32[]{:S(2)}, u32[]{:S(2)}) %collective-permute-start.17) | collective-permute-done | bytes 65568 | tf_op jit(solution)/shard_map/ppermute | solution.py:335
  72.2 2.7 %collective-permute-done.16.from_left = f32[128,128]{1,0:T(8,128)S(1)} collective-permute-done((f32[128,128]{1,0:T(8,128)S(1)}, f32[128,128]{1,0:T(8,128)S(1)}, u32[]{:S(2)}, u32[]{:S(2)}) %collective-permute-start.16) | collective-permute-done | bytes 65568 | tf_op jit(solution)/shard_map/ppermute | solution.py:335
  74.9 0.1 shard_map.87.refs_0_
  75.0 1.8 %collective-permute-start.20 = (f32[128,128]{1,0:T(8,128)S(1)}, f32[128,128]{1,0:T(8,128)S(1)}, u32[]{:S(2)}, u32[]{:S(2)}) collective-permute-start(f32[128,128]{1,0:T(8,128)S(1)} %shard_map.87.refs_0_), channel_id=1, source_target_pairs={{0,3},{1,2},{2,1},{3,0},{4,7},{5,6},{6,5},{7,4},{8,11},{9,10},{10,... | collective-permute-start | bytes 196616 | tf_op jit(solution)/shard_map/ppermute | solution.py:330
  76.8 0.0 collective-permute-start.19
  76.8 2.7 %collective-permute-start.18 = (f32[128,128]{1,0:T(8,128)S(1)}, f32[128,128]{1,0:T(8,128)S(1)}, u32[]{:S(2)}, u32[]{:S(2)}) collective-permute-start(f32[128,128]{1,0:T(8,128)S(1)} %shard_map.87.refs_0_), channel_id=1, source_target_pairs={{0,1},{1,0},{2,3},{3,2},{4,5},{5,4},{6,7},{7,6},{8,9},{9,8},{10,11... | collective-permute-start | bytes 196616 | tf_op jit(solution)/shard_map/ppermute | solution.py:330
  79.5 0.7 shard_map.89
  80.2 1.5 %collective-permute-done.20.refs_3_ = f32[128,128]{1,0:T(8,128)S(1)} collective-permute-done((f32[128,128]{1,0:T(8,128)S(1)}, f32[128,128]{1,0:T(8,128)S(1)}, u32[]{:S(2)}, u32[]{:S(2)}) %collective-permute-start.20) | collective-permute-done | bytes 65568 | tf_op jit(solution)/shard_map/ppermute | solution.py:330
  81.7 1.1 %collective-permute-done.19.refs_2_ = f32[128,128]{1,0:T(8,128)S(1)} collective-permute-done((f32[128,128]{1,0:T(8,128)S(1)}, f32[128,128]{1,0:T(8,128)S(1)}, u32[]{:S(2)}, u32[]{:S(2)}) %collective-permute-start.19) | collective-permute-done | bytes 65568 | tf_op jit(solution)/shard_map/ppermute | solution.py:330
  82.8 0.0 collective-permute-done.18.refs_1_
  82.8 0.7 shard_map.88
  (6 shorter events, 0.0 us)
Async XLA Ops:
  0.6 15.3 %collective-permute-start.2 = (f32[4,2,128,128]{3,2,1,0:T(8,128)}, f32[4,2,128,128]{3,2,1,0:T(8,128)S(1)}, u32[]{:S(2)}, u32[]{:S(2)}) collective-permute-start(f32[4,2,128,128]{3,2,1,0:T(8,128)} %probe.1), channel_id=1, source_target_pairs={{0,1},{1,0},{2,3},{3,2},{4,5},{5,4},{6,7},{7,6},{8,9},{9,8},{10,11... | collective-permute-start | bytes 1572872 | tf_op jit(solution)/shard_map/ppermute | solution.py:330
  3.7 0.9 %copy-start.3 = (f32[1,2,2,128,128]{4,3,2,1,0:T(8,128)S(1)}, f32[1,2,2,128,128]{4,3,2,1,0:T(8,128)}, u32[]{:S(2)}) copy-start(f32[1,2,2,128,128]{4,3,2,1,0:T(8,128)} %param.6) | copy-start | bytes 786436
  4.8 5.3 %collective-permute-start = (f32[2,128,128]{2,1,0:T(8,128)S(1)}, f32[2,128,128]{2,1,0:T(8,128)S(1)}, u32[]{:S(2)}, u32[]{:S(2)}) collective-permute-start(f32[2,128,128]{2,1,0:T(8,128)S(1)} %get-tuple-element.34), channel_id=1, source_target_pairs={{0,4},{4,8},{8,12},{12,16},{16,20},{20,24},{24,28},{28,0},{1,5},{5... | collective-permute-start | bytes 393224 | tf_op jit(solution)/shard_map/ppermute | solution.py:335
  4.9 5.3 %collective-permute-start.1 = (f32[2,128,128]{2,1,0:T(8,128)S(1)}, f32[2,128,128]{2,1,0:T(8,128)S(1)}, u32[]{:S(2)}, u32[]{:S(2)}) collective-permute-start(f32[2,128,128]{2,1,0:T(8,128)S(1)} %get-tuple-element.35), channel_id=1, source_target_pairs={{0,28},{4,0},{8,4},{12,8},{16,12},{20,16},{24,20},{28,24},{1,29},{... | collective-permute-start | bytes 393224 | tf_op jit(solution)/shard_map/ppermute | solution.py:335
  7.5 1.0 %copy-start.2 = (f32[4,2,128,128]{3,2,1,0:T(8,128)S(1)}, f32[4,2,128,128]{3,2,1,0:T(8,128)}, u32[]{:S(2)}) copy-start(f32[4,2,128,128]{3,2,1,0:T(8,128)} %probe.1) | copy-start | bytes 1572868
  8.6 0.7 copy-start.5
  8.6 0.9 %copy-start.4 = (f32[128,128]{1,0:T(8,128)S(1)}, f32[128,128]{1,0:T(8,128)}, u32[]{:S(2)}) copy-start(f32[128,128]{1,0:T(8,128)} %param.8) | copy-start | bytes 196612
  8.6 1.6 %copy-start = (bf16[2,256,256]{2,1,0:T(8,128)(2,1)S(1)}, bf16[2,256,256]{2,1,0:T(8,128)(2,1)}, u32[]{:S(2)}) copy-start(bf16[2,256,256]{2,1,0:T(8,128)(2,1)} %constant.6.clone.refs_6_.table.refs_9_.refs_7_) | copy-start | bytes 786436
  15.9 7.4 %copy-start.1 = (f32[4,128,128]{2,1,0:T(8,128)S(1)}, f32[4,128,128]{2,1,0:T(8,128)}, u32[]{:S(2)}) copy-start(f32[4,128,128]{2,1,0:T(8,128)} %refs_2_.3) | copy-start | bytes 786436
  18.1 5.2 %collective-permute-start.3 = (f32[128,128]{1,0:T(8,128)S(1)}, f32[128,128]{1,0:T(8,128)S(1)}, u32[]{:S(2)}, u32[]{:S(2)}) collective-permute-start(f32[128,128]{1,0:T(8,128)S(1)} %get-tuple-element.40.refs_0_), channel_id=1, source_target_pairs={{0,2},{1,3},{2,0},{3,1},{4,6},{5,7},{6,4},{7,5},{8,10},{9,11},{10,... | collective-permute-start | bytes 196616 | tf_op jit(solution)/shard_map/ppermute | solution.py:330
  26.1 11.0 %collective-permute-start.4 = (f32[2,128,128]{2,1,0:T(8,128)S(1)}, f32[2,128,128]{2,1,0:T(8,128)S(1)}, u32[]{:S(2)}, u32[]{:S(2)}) collective-permute-start(f32[2,128,128]{2,1,0:T(8,128)S(1)} %get-tuple-element.45.refs_0_), channel_id=1, source_target_pairs={{0,1},{1,0},{2,3},{3,2},{4,5},{5,4},{6,7},{7,6},{8,9},{9,8},{10,11... | collective-permute-start | bytes 393224 | tf_op jit(solution)/shard_map/ppermute | solution.py:330
  27.9 6.0 %collective-permute-start.5 = (f32[128,128]{1,0:T(8,128)S(1)}, f32[128,128]{1,0:T(8,128)S(1)}, u32[]{:S(2)}, u32[]{:S(2)}) collective-permute-start(f32[128,128]{1,0:T(8,128)S(1)} %get-tuple-element.46), channel_id=1, source_target_pairs={{0,2},{1,3},{2,0},{3,1},{4,6},{5,7},{6,4},{7,5},{8,10},{9,11},{10,... | collective-permute-start | bytes 196616 | tf_op jit(solution)/shard_map/ppermute | solution.py:330
  31.1 6.1 %collective-permute-start.6 = (f32[128,128]{1,0:T(8,128)S(1)}, f32[128,128]{1,0:T(8,128)S(1)}, u32[]{:S(2)}, u32[]{:S(2)}) collective-permute-start(f32[128,128]{1,0:T(8,128)S(1)} %get-tuple-element.47), channel_id=1, source_target_pairs={{0,3},{1,2},{2,1},{3,0},{4,7},{5,6},{6,5},{7,4},{8,11},{9,10},{10,... | collective-permute-start | bytes 196616 | tf_op jit(solution)/shard_map/ppermute | solution.py:330
  37.5 2.0 %collective-permute-start.8 = (f32[128,128]{1,0:T(8,128)S(1)}, f32[128,128]{1,0:T(8,128)S(1)}, u32[]{:S(2)}, u32[]{:S(2)}) collective-permute-start(f32[128,128]{1,0:T(8,128)S(1)} %get-tuple-element.48.left), channel_id=1, source_target_pairs={{0,28},{4,0},{8,4},{12,8},{16,12},{20,16},{24,20},{28,24},{1,29},{... | collective-permute-start | bytes 196616 | tf_op jit(solution)/shard_map/ppermute | solution.py:335
  37.6 5.4 %collective-permute-start.7 = (f32[128,128]{1,0:T(8,128)S(1)}, f32[128,128]{1,0:T(8,128)S(1)}, u32[]{:S(2)}, u32[]{:S(2)}) collective-permute-start(f32[128,128]{1,0:T(8,128)S(1)} %get-tuple-element.49.right), channel_id=1, source_target_pairs={{0,4},{4,8},{8,12},{12,16},{16,20},{20,24},{24,28},{28,0},{1,5},{5... | collective-permute-start | bytes 196616 | tf_op jit(solution)/shard_map/ppermute | solution.py:335
  43.2 5.2 %collective-permute-start.10 = (f32[128,128]{1,0:T(8,128)S(1)}, f32[128,128]{1,0:T(8,128)S(1)}, u32[]{:S(2)}, u32[]{:S(2)}) collective-permute-start(f32[128,128]{1,0:T(8,128)S(1)} %get-tuple-element.51.refs_0_), channel_id=1, source_target_pairs={{0,2},{1,3},{2,0},{3,1},{4,6},{5,7},{6,4},{7,5},{8,10},{9,11},{10,... | collective-permute-start | bytes 196616 | tf_op jit(solution)/shard_map/ppermute | solution.py:330
  43.4 6.2 %collective-permute-start.11 = (f32[128,128]{1,0:T(8,128)S(1)}, f32[128,128]{1,0:T(8,128)S(1)}, u32[]{:S(2)}, u32[]{:S(2)}) collective-permute-start(f32[128,128]{1,0:T(8,128)S(1)} %get-tuple-element.52), channel_id=1, source_target_pairs={{0,3},{1,2},{2,1},{3,0},{4,7},{5,6},{6,5},{7,4},{8,11},{9,10},{10,... | collective-permute-start | bytes 196616 | tf_op jit(solution)/shard_map/ppermute | solution.py:330
  44.6 5.2 %collective-permute-start.9 = (f32[128,128]{1,0:T(8,128)S(1)}, f32[128,128]{1,0:T(8,128)S(1)}, u32[]{:S(2)}, u32[]{:S(2)}) collective-permute-start(f32[128,128]{1,0:T(8,128)S(1)} %get-tuple-element.52), channel_id=1, source_target_pairs={{0,1},{1,0},{2,3},{3,2},{4,5},{5,4},{6,7},{7,6},{8,9},{9,8},{10,11... | collective-permute-start | bytes 196616 | tf_op jit(solution)/shard_map/ppermute | solution.py:330
  52.7 5.2 %collective-permute-start.12 = (f32[128,128]{1,0:T(8,128)S(1)}, f32[128,128]{1,0:T(8,128)S(1)}, u32[]{:S(2)}, u32[]{:S(2)}) collective-permute-start(f32[128,128]{1,0:T(8,128)S(1)} %get-tuple-element.53.refs_0_), channel_id=1, source_target_pairs={{0,2},{1,3},{2,0},{3,1},{4,6},{5,7},{6,4},{7,5},{8,10},{9,11},{10,... | collective-permute-start | bytes 196616 | tf_op jit(solution)/shard_map/ppermute | solution.py:330
  60.8 9.1 %collective-permute-start.13 = (f32[2,128,128]{2,1,0:T(8,128)S(1)}, f32[2,128,128]{2,1,0:T(8,128)S(1)}, u32[]{:S(2)}, u32[]{:S(2)}) collective-permute-start(f32[2,128,128]{2,1,0:T(8,128)S(1)} %get-tuple-element.58.refs_2_), channel_id=1, source_target_pairs={{0,1},{1,0},{2,3},{3,2},{4,5},{5,4},{6,7},{7,6},{8,9},{9,8},{10,11... | collective-permute-start | bytes 393224 | tf_op jit(solution)/shard_map/ppermute | solution.py:330
  62.1 5.9 %collective-permute-start.14 = (f32[128,128]{1,0:T(8,128)S(1)}, f32[128,128]{1,0:T(8,128)S(1)}, u32[]{:S(2)}, u32[]{:S(2)}) collective-permute-start(f32[128,128]{1,0:T(8,128)S(1)} %get-tuple-element.59), channel_id=1, source_target_pairs={{0,2},{1,3},{2,0},{3,1},{4,6},{5,7},{6,4},{7,5},{8,10},{9,11},{10,... | collective-permute-start | bytes 196616 | tf_op jit(solution)/shard_map/ppermute | solution.py:330
  63.8 6.1 %collective-permute-start.15 = (f32[128,128]{1,0:T(8,128)S(1)}, f32[128,128]{1,0:T(8,128)S(1)}, u32[]{:S(2)}, u32[]{:S(2)}) collective-permute-start(f32[128,128]{1,0:T(8,128)S(1)} %get-tuple-element.60), channel_id=1, source_target_pairs={{0,3},{1,2},{2,1},{3,0},{4,7},{5,6},{6,5},{7,4},{8,11},{9,10},{10,... | collective-permute-start | bytes 196616 | tf_op jit(solution)/shard_map/ppermute | solution.py:330
  70.2 2.0 %collective-permute-start.17 = (f32[128,128]{1,0:T(8,128)S(1)}, f32[128,128]{1,0:T(8,128)S(1)}, u32[]{:S(2)}, u32[]{:S(2)}) collective-permute-start(f32[128,128]{1,0:T(8,128)S(1)} %get-tuple-element.61.left), channel_id=1, source_target_pairs={{0,28},{4,0},{8,4},{12,8},{16,12},{20,16},{24,20},{28,24},{1,29},{... | collective-permute-start | bytes 196616 | tf_op jit(solution)/shard_map/ppermute | solution.py:335
  70.3 4.6 %collective-permute-start.16 = (f32[128,128]{1,0:T(8,128)S(1)}, f32[128,128]{1,0:T(8,128)S(1)}, u32[]{:S(2)}, u32[]{:S(2)}) collective-permute-start(f32[128,128]{1,0:T(8,128)S(1)} %get-tuple-element.62.right), channel_id=1, source_target_pairs={{0,4},{4,8},{8,12},{12,16},{16,20},{20,24},{24,28},{28,0},{1,5},{5... | collective-permute-start | bytes 196616 | tf_op jit(solution)/shard_map/ppermute | solution.py:335
  75.0 6.7 %collective-permute-start.20 = (f32[128,128]{1,0:T(8,128)S(1)}, f32[128,128]{1,0:T(8,128)S(1)}, u32[]{:S(2)}, u32[]{:S(2)}) collective-permute-start(f32[128,128]{1,0:T(8,128)S(1)} %shard_map.87.refs_0_), channel_id=1, source_target_pairs={{0,3},{1,2},{2,1},{3,0},{4,7},{5,6},{6,5},{7,4},{8,11},{9,10},{10,... | collective-permute-start | bytes 196616 | tf_op jit(solution)/shard_map/ppermute | solution.py:330
  76.8 6.1 %collective-permute-start.19 = (f32[128,128]{1,0:T(8,128)S(1)}, f32[128,128]{1,0:T(8,128)S(1)}, u32[]{:S(2)}, u32[]{:S(2)}) collective-permute-start(f32[128,128]{1,0:T(8,128)S(1)} %shard_map.87.refs_0_), channel_id=1, source_target_pairs={{0,2},{1,3},{2,0},{3,1},{4,6},{5,7},{6,4},{7,5},{8,10},{9,11},{10,... | collective-permute-start | bytes 196616 | tf_op jit(solution)/shard_map/ppermute | solution.py:330
  76.8 6.1 %collective-permute-start.18 = (f32[128,128]{1,0:T(8,128)S(1)}, f32[128,128]{1,0:T(8,128)S(1)}, u32[]{:S(2)}, u32[]{:S(2)}) collective-permute-start(f32[128,128]{1,0:T(8,128)S(1)} %shard_map.87.refs_0_), channel_id=1, source_target_pairs={{0,1},{1,0},{2,3},{3,2},{4,5},{5,4},{6,7},{7,6},{8,9},{9,8},{10,11... | collective-permute-start | bytes 196616 | tf_op jit(solution)/shard_map/ppermute | solution.py:330

commit v2 on v1

--- a/solution.py
+++ b/solution.py
@@ -12,7 +12,6 @@
 STEPS = 2
 TILE_COLS = 8
 SUB = 8
-CHAIN = 2
 
 learning_rate = 0.5
 
@@ -67,8 +66,8 @@
 
 
 def dft(waves, high, low):
-    k = waves[0].shape[0]
-    chains = [jnp.concatenate(waves[i : i + CHAIN], axis=0) for i in range(0, len(waves), CHAIN)]
+    k, size = waves[0].shape[0], max(1, len(waves) // 4)
+    chains = [jnp.concatenate(waves[i : i + size], axis=0) for i in range(0, len(waves), size)]
     chains = [product(x, high, low) for x in chains]
     chains = [flip(x, k) for x in chains]
     chains = [product(x, high, low) for x in chains]

time: 83.8 us -> 83.3 us (level)
  no operation moved by 1% of the time
where the time goes in v2:
time: 83.3 us; the launch traced here: 83.1 us
  waiting for transfers between devices  36 us (43%)
  starting transfers between devices  28.1 us (34%)
  Pallas kernels  15.1 us (18%)
  local copies, waits for them, and re-layouts  3.13 us (4%)
    ppermute x15, waiting for transfers between devices, across(): lax.ppermute(value, axis, [(i, i ^ bits) for i in range(lax.axis_size(axi...  26.6 us
    ppermute x15, starting transfers between devices, across(): lax.ppermute(value, axis, [(i, i ^ bits) for i in range(lax.axis_size(axi...  24.3 us
    pallas_call x13, Pallas kernels, call(): pl.pallas_call(body, out_shape=[jax.ShapeDtypeStruct(s, f32) for s in out...  15.1 us
    ppermute x6, waiting for transfers between devices, around(): lax.ppermute(value, 'tile', [(i, (i + steps) % count) for i in range(coun...  9.43 us
    ppermute x6, starting transfers between devices, around(): lax.ppermute(value, 'tile', [(i, (i + steps) % count) for i in range(coun...  3.8 us
    unnamed x14, local copies, waits for them, and re-layouts  2.89 us
  transfers between devices with their start and end apart: 21, of which 17 were waited for; matrix products, arithmetic and copies ran while one was open for 1% of the time, Pallas kernels for 4%

profile of v2, /device:TPU:0, one launch (start us, length us, event | category | flops | bytes accessed | tf_op | source)
XLA Modules:
  0.0 83.1 jit_solution(5166067298150094759)
XLA Ops:
  0.6 3.1 %collective-permute-start.2 = (f32[4,2,128,128]{3,2,1,0:T(8,128)}, f32[4,2,128,128]{3,2,1,0:T(8,128)S(1)}, u32[]{:S(2)}, u32[]{:S(2)}) collective-permute-start(f32[4,2,128,128]{3,2,1,0:T(8,128)} %probe.1), channel_id=1, source_target_pairs={{0,1},{1,0},{2,3},{3,2},{4,5},{5,4},{6,7},{7,6},{8,9},{9,8},{10,11... | collective-permute-start | bytes 1572872 | tf_op jit(solution)/shard_map/ppermute | solution.py:329
  3.7 0.9 %copy-done.3 = f32[1,2,2,128,128]{4,3,2,1,0:T(8,128)S(1)} copy-done((f32[1,2,2,128,128]{4,3,2,1,0:T(8,128)S(1)}, f32[1,2,2,128,128]{4,3,2,1,0:T(8,128)}, u32[]{:S(2)}) %copy-start.3) | copy-done | bytes 262168
  4.7 0.1 shard_map.77
  4.8 0.1 collective-permute-start
  4.9 2.6 %collective-permute-start.1 = (f32[2,128,128]{2,1,0:T(8,128)S(1)}, f32[2,128,128]{2,1,0:T(8,128)S(1)}, u32[]{:S(2)}, u32[]{:S(2)}) collective-permute-start(f32[2,128,128]{2,1,0:T(8,128)S(1)} %get-tuple-element.35), channel_id=1, source_target_pairs={{0,28},{4,0},{8,4},{12,8},{16,12},{20,16},{24,20},{28,24},{1,29},{... | collective-permute-start | bytes 393224 | tf_op jit(solution)/shard_map/ppermute | solution.py:334
  7.5 1.0 %copy-done.2 = f32[4,2,128,128]{3,2,1,0:T(8,128)S(1)} copy-done((f32[4,2,128,128]{3,2,1,0:T(8,128)S(1)}, f32[4,2,128,128]{3,2,1,0:T(8,128)}, u32[]{:S(2)}) %copy-start.2) | copy-done | bytes 524312
  8.6 0.0 copy-start
  8.6 0.6 copy-done.5
  9.3 0.1 copy.16.pos
  9.3 0.1 copy-done.4
  9.4 0.1 copy.11
  9.5 0.2 sine_bitcast_fusion
  9.8 0.4 collective-permute-done.refs_1_
  10.2 0.0 collective-permute-done.1.refs_2_
  10.2 0.0 copy-done
  10.2 2.3 %shard_map.79 = (f32[4,128,128]{2,1,0:T(8,128)S(1)}, f32[264,256]{1,0:T(8,128)S(1)}, f32[128,128]{1,0:T(8,128)S(1)}, f32[8,128,256]{2,1,0:T(8,128)S(1)}, f32[8,128,256]{2,1,0:T(8,128)S(1)}) custom-call(s32[1]{0:T(128)} %bitcast.index, s32[4,2]{1,0:T(4,128)S(1)} %copy.16.pos, f32[4,128,128]{2,1,0:T(8,128)S(1)} %get-tuple-element.33.refs_0_, ...), custom_call_target="tpu_custom_call" | custom-call | tf_op jit(solution)/shard_map/pallas_call | solution.py:38
  12.4 3.4 %collective-permute-done.2.probe = f32[4,2,128,128]{3,2,1,0:T(8,128)S(1)} collective-permute-done((f32[4,2,128,128]{3,2,1,0:T(8,128)}, f32[4,2,128,128]{3,2,1,0:T(8,128)S(1)}, u32[]{:S(2)}, u32[]{:S(2)}) %collective-permute-start.2) | collective-permute-done | bytes 524320 | tf_op jit(solution)/shard_map/ppermute | solution.py:329
  15.9 1.7 %shard_map.80 = (f32[128,128]{1,0:T(8,128)S(1)}, f32[8,2,128,128]{3,2,1,0:T(8,128)S(1)}, f32[8,128,256]{2,1,0:T(8,128)S(1)}, f32[8,128,256]{2,1,0:T(8,128)S(1)}) custom-call(f32[4,128,128]{2,1,0:T(8,128)S(1)} %get-tuple-element.36.win.refs_3_, ...), custom_call_target="tpu_custom_call", output_to_operand_aliasing={{1}: (6, {}), {2}: (7, {}), {3}: (8, {})} | custom-call | tf_op jit(solution)/shard_map/pallas_call | solution.py:38
  17.6 2.8 %collective-permute-start.3 = (f32[128,128]{1,0:T(8,128)S(1)}, f32[128,128]{1,0:T(8,128)S(1)}, u32[]{:S(2)}, u32[]{:S(2)}) collective-permute-start(f32[128,128]{1,0:T(8,128)S(1)} %get-tuple-element.40.refs_0_), channel_id=1, source_target_pairs={{0,2},{1,3},{2,0},{3,1},{4,6},{5,7},{6,4},{7,5},{8,10},{9,11},{10,... | collective-permute-start | bytes 196616 | tf_op jit(solution)/shard_map/ppermute | solution.py:329
  20.5 2.4 %collective-permute-done.3.refs_1_ = f32[128,128]{1,0:T(8,128)S(1)} collective-permute-done((f32[128,128]{1,0:T(8,128)S(1)}, f32[128,128]{1,0:T(8,128)S(1)}, u32[]{:S(2)}, u32[]{:S(2)}) %collective-permute-start.3) | collective-permute-done | bytes 65568 | tf_op jit(solution)/shard_map/ppermute | solution.py:329
  22.9 0.0 copy-done.1
  22.9 2.8 %shard_map.81 = (f32[128,128]{1,0:T(8,128)S(1)}, f32[2,128,128]{2,1,0:T(8,128)S(1)}, f32[128,128]{1,0:T(8,128)S(1)}, f32[128,128]{1,0:T(8,128)S(1)}) custom-call(s32[1]{0:T(128)} %bitcast.index, f32[128,128]{1,0:T(8,128)S(1)} %get-tuple-element.40.refs_0_, f32[128,128]{1,0:T(8,128)S(1)} %collective-permute-done.3.refs_1_, f32[4,128,128]{2,1,0:T(8,128)S(1)} %copy-done.1, ...), custom_call_target="tpu_custom_call" | custom-call | tf_op jit(solution)/shard_map/pallas_call | solution.py:38
  25.7 1.8 %collective-permute-start.4 = (f32[2,128,128]{2,1,0:T(8,128)S(1)}, f32[2,128,128]{2,1,0:T(8,128)S(1)}, u32[]{:S(2)}, u32[]{:S(2)}) collective-permute-start(f32[2,128,128]{2,1,0:T(8,128)S(1)} %get-tuple-element.45.refs_0_), channel_id=1, source_target_pairs={{0,1},{1,0},{2,3},{3,2},{4,5},{5,4},{6,7},{7,6},{8,9},{9,8},{10,11... | collective-permute-start | bytes 393224 | tf_op jit(solution)/shard_map/ppermute | solution.py:329
  27.5 3.2 %collective-permute-start.5 = (f32[128,128]{1,0:T(8,128)S(1)}, f32[128,128]{1,0:T(8,128)S(1)}, u32[]{:S(2)}, u32[]{:S(2)}) collective-permute-start(f32[128,128]{1,0:T(8,128)S(1)} %get-tuple-element.46), channel_id=1, source_target_pairs={{0,2},{1,3},{2,0},{3,1},{4,6},{5,7},{6,4},{7,5},{8,10},{9,11},{10,... | collective-permute-start | bytes 196616 | tf_op jit(solution)/shard_map/ppermute | solution.py:329
  30.7 0.0 collective-permute-start.6
  30.7 2.8 %collective-permute-done.5.refs_2_ = f32[128,128]{1,0:T(8,128)S(1)} collective-permute-done((f32[128,128]{1,0:T(8,128)S(1)}, f32[128,128]{1,0:T(8,128)S(1)}, u32[]{:S(2)}, u32[]{:S(2)}) %collective-permute-start.5) | collective-permute-done | bytes 65568 | tf_op jit(solution)/shard_map/ppermute | solution.py:329
  33.5 3.2 %collective-permute-done.6.refs_3_ = f32[128,128]{1,0:T(8,128)S(1)} collective-permute-done((f32[128,128]{1,0:T(8,128)S(1)}, f32[128,128]{1,0:T(8,128)S(1)}, u32[]{:S(2)}, u32[]{:S(2)}) %collective-permute-start.6) | collective-permute-done | bytes 65568 | tf_op jit(solution)/shard_map/ppermute | solution.py:329
  36.7 0.0 collective-permute-done.4.refs_1_
  36.7 0.3 shard_map.82
  37.1 0.1 collective-permute-start.8
  37.1 0.5 collective-permute-start.7
  37.6 1.4 %collective-permute-done.8.from_right = f32[128,128]{1,0:T(8,128)S(1)} collective-permute-done((f32[128,128]{1,0:T(8,128)S(1)}, f32[128,128]{1,0:T(8,128)S(1)}, u32[]{:S(2)}, u32[]{:S(2)}) %collective-permute-start.8) | collective-permute-done | bytes 65568 | tf_op jit(solution)/shard_map/ppermute | solution.py:334
  39.0 3.5 %collective-permute-done.7.from_left = f32[128,128]{1,0:T(8,128)S(1)} collective-permute-done((f32[128,128]{1,0:T(8,128)S(1)}, f32[128,128]{1,0:T(8,128)S(1)}, u32[]{:S(2)}, u32[]{:S(2)}) %collective-permute-start.7) | collective-permute-done | bytes 65568 | tf_op jit(solution)/shard_map/ppermute | solution.py:334
  42.5 0.3 shard_map.83
  42.8 0.2 collective-permute-start.10
  42.9 1.3 %collective-permute-start.11 = (f32[128,128]{1,0:T(8,128)S(1)}, f32[128,128]{1,0:T(8,128)S(1)}, u32[]{:S(2)}, u32[]{:S(2)}) collective-permute-start(f32[128,128]{1,0:T(8,128)S(1)} %get-tuple-element.52), channel_id=1, source_target_pairs={{0,3},{1,2},{2,1},{3,0},{4,7},{5,6},{6,5},{7,4},{8,11},{9,10},{10,... | collective-permute-start | bytes 196616 | tf_op jit(solution)/shard_map/ppermute | solution.py:329
  44.2 2.1 %collective-permute-start.9 = (f32[128,128]{1,0:T(8,128)S(1)}, f32[128,128]{1,0:T(8,128)S(1)}, u32[]{:S(2)}, u32[]{:S(2)}) collective-permute-start(f32[128,128]{1,0:T(8,128)S(1)} %get-tuple-element.52), channel_id=1, source_target_pairs={{0,1},{1,0},{2,3},{3,2},{4,5},{5,4},{6,7},{7,6},{8,9},{9,8},{10,11... | collective-permute-start | bytes 196616 | tf_op jit(solution)/shard_map/ppermute | solution.py:329
  46.4 1.7 %collective-permute-done.10.refs_2_ = f32[128,128]{1,0:T(8,128)S(1)} collective-permute-done((f32[128,128]{1,0:T(8,128)S(1)}, f32[128,128]{1,0:T(8,128)S(1)}, u32[]{:S(2)}, u32[]{:S(2)}) %collective-permute-start.10) | collective-permute-done | bytes 65568 | tf_op jit(solution)/shard_map/ppermute | solution.py:329
  48.0 1.1 %collective-permute-done.11.refs_3_ = f32[128,128]{1,0:T(8,128)S(1)} collective-permute-done((f32[128,128]{1,0:T(8,128)S(1)}, f32[128,128]{1,0:T(8,128)S(1)}, u32[]{:S(2)}, u32[]{:S(2)}) %collective-permute-start.11) | collective-permute-done | bytes 65568 | tf_op jit(solution)/shard_map/ppermute | solution.py:329
  49.1 0.3 collective-permute-done.9.refs_1_
  49.4 2.8 %shard_map.84 = (f32[4,128,128]{2,1,0:T(8,128)S(1)}, f32[128,128]{1,0:T(8,128)S(1)}, f32[8,128,256]{2,1,0:T(8,128)S(1)}, f32[8,128,256]{2,1,0:T(8,128)S(1)}) custom-call(s32[1]{0:T(128)} %bitcast.index, f32[128,128]{1,0:T(8,128)S(1)} %get-tuple-element.51.refs_0_, f32[128,128]{1,0:T(8,128)S(1)} %collective-permute-done.9.refs_1_, ...), custom_call_target="tpu_custom_call" | custom-call | tf_op jit(solution)/shard_map/pallas_call | solution.py:38
  52.3 0.9 %collective-permute-start.12 = (f32[128,128]{1,0:T(8,128)S(1)}, f32[128,128]{1,0:T(8,128)S(1)}, u32[]{:S(2)}, u32[]{:S(2)}) collective-permute-start(f32[128,128]{1,0:T(8,128)S(1)} %get-tuple-element.53.refs_0_), channel_id=1, source_target_pairs={{0,2},{1,3},{2,0},{3,1},{4,6},{5,7},{6,4},{7,5},{8,10},{9,11},{10,... | collective-permute-start | bytes 196616 | tf_op jit(solution)/shard_map/ppermute | solution.py:329
  53.2 4.3 %collective-permute-done.12.refs_1_ = f32[128,128]{1,0:T(8,128)S(1)} collective-permute-done((f32[128,128]{1,0:T(8,128)S(1)}, f32[128,128]{1,0:T(8,128)S(1)}, u32[]{:S(2)}, u32[]{:S(2)}) %collective-permute-start.12) | collective-permute-done | bytes 65568 | tf_op jit(solution)/shard_map/ppermute | solution.py:329
  57.5 2.9 %shard_map.85 = (f32[128,128]{1,0:T(8,128)S(1)}, f32[2,128,128]{2,1,0:T(8,128)S(1)}, f32[128,128]{1,0:T(8,128)S(1)}, f32[128,128]{1,0:T(8,128)S(1)}) custom-call(s32[1]{0:T(128)} %bitcast.index, f32[128,128]{1,0:T(8,128)S(1)} %get-tuple-element.53.refs_0_, f32[128,128]{1,0:T(8,128)S(1)} %collective-permute-done.12.refs_1_, f32[4,128,128]{2,1,0:T(8,128)S(1)} %copy-done.1, ...), custom_call_target="tpu_custom_call" | custom-call | tf_op jit(solution)/shard_map/pallas_call | solution.py:38
  60.4 1.3 %collective-permute-start.13 = (f32[2,128,128]{2,1,0:T(8,128)S(1)}, f32[2,128,128]{2,1,0:T(8,128)S(1)}, u32[]{:S(2)}, u32[]{:S(2)}) collective-permute-start(f32[2,128,128]{2,1,0:T(8,128)S(1)} %get-tuple-element.58.refs_2_), channel_id=1, source_target_pairs={{0,1},{1,0},{2,3},{3,2},{4,5},{5,4},{6,7},{7,6},{8,9},{9,8},{10,11... | collective-permute-start | bytes 393224 | tf_op jit(solution)/shard_map/ppermute | solution.py:329
  61.7 1.7 %collective-permute-start.14 = (f32[128,128]{1,0:T(8,128)S(1)}, f32[128,128]{1,0:T(8,128)S(1)}, u32[]{:S(2)}, u32[]{:S(2)}) collective-permute-start(f32[128,128]{1,0:T(8,128)S(1)} %get-tuple-element.59), channel_id=1, source_target_pairs={{0,2},{1,3},{2,0},{3,1},{4,6},{5,7},{6,4},{7,5},{8,10},{9,11},{10,... | collective-permute-start | bytes 196616 | tf_op jit(solution)/shard_map/ppermute | solution.py:329
  63.4 1.4 %collective-permute-start.15 = (f32[128,128]{1,0:T(8,128)S(1)}, f32[128,128]{1,0:T(8,128)S(1)}, u32[]{:S(2)}, u32[]{:S(2)}) collective-permute-start(f32[128,128]{1,0:T(8,128)S(1)} %get-tuple-element.60), channel_id=1, source_target_pairs={{0,3},{1,2},{2,1},{3,0},{4,7},{5,6},{6,5},{7,4},{8,11},{9,10},{10,... | collective-permute-start | bytes 196616 | tf_op jit(solution)/shard_map/ppermute | solution.py:329
  64.8 2.7 %collective-permute-done.14.refs_2_ = f32[128,128]{1,0:T(8,128)S(1)} collective-permute-done((f32[128,128]{1,0:T(8,128)S(1)}, f32[128,128]{1,0:T(8,128)S(1)}, u32[]{:S(2)}, u32[]{:S(2)}) %collective-permute-start.14) | collective-permute-done | bytes 65568 | tf_op jit(solution)/shard_map/ppermute | solution.py:329
  67.5 1.9 %collective-permute-done.15.refs_3_ = f32[128,128]{1,0:T(8,128)S(1)} collective-permute-done((f32[128,128]{1,0:T(8,128)S(1)}, f32[128,128]{1,0:T(8,128)S(1)}, u32[]{:S(2)}, u32[]{:S(2)}) %collective-permute-start.15) | collective-permute-done | bytes 65568 | tf_op jit(solution)/shard_map/ppermute | solution.py:329
  69.4 0.0 collective-permute-done.13.refs_1_.refs_3_
  69.4 0.3 shard_map.86
  69.8 0.1 collective-permute-start.17
  69.8 0.5 collective-permute-start.16
  70.3 1.5 %collective-permute-done.17.from_right = f32[128,128]{1,0:T(8,128)S(1)} collective-permute-done((f32[128,128]{1,0:T(8,128)S(1)}, f32[128,128]{1,0:T(8,128)S(1)}, u32[]{:S(2)}, u32[]{:S(2)}) %collective-permute-start.17) | collective-permute-done | bytes 65568 | tf_op jit(solution)/shard_map/ppermute | solution.py:334
  71.8 2.7 %collective-permute-done.16.from_left = f32[128,128]{1,0:T(8,128)S(1)} collective-permute-done((f32[128,128]{1,0:T(8,128)S(1)}, f32[128,128]{1,0:T(8,128)S(1)}, u32[]{:S(2)}, u32[]{:S(2)}) %collective-permute-start.16) | collective-permute-done | bytes 65568 | tf_op jit(solution)/shard_map/ppermute | solution.py:334
  74.5 0.1 shard_map.87.refs_0_
  74.6 1.8 %collective-permute-start.20 = (f32[128,128]{1,0:T(8,128)S(1)}, f32[128,128]{1,0:T(8,128)S(1)}, u32[]{:S(2)}, u32[]{:S(2)}) collective-permute-start(f32[128,128]{1,0:T(8,128)S(1)} %shard_map.87.refs_0_), channel_id=1, source_target_pairs={{0,3},{1,2},{2,1},{3,0},{4,7},{5,6},{6,5},{7,4},{8,11},{9,10},{10,... | collective-permute-start | bytes 196616 | tf_op jit(solution)/shard_map/ppermute | solution.py:329
  76.3 0.0 collective-permute-start.19
  76.3 2.7 %collective-permute-start.18 = (f32[128,128]{1,0:T(8,128)S(1)}, f32[128,128]{1,0:T(8,128)S(1)}, u32[]{:S(2)}, u32[]{:S(2)}) collective-permute-start(f32[128,128]{1,0:T(8,128)S(1)} %shard_map.87.refs_0_), channel_id=1, source_target_pairs={{0,1},{1,0},{2,3},{3,2},{4,5},{5,4},{6,7},{7,6},{8,9},{9,8},{10,11... | collective-permute-start | bytes 196616 | tf_op jit(solution)/shard_map/ppermute | solution.py:329
  79.0 0.7 shard_map.89
  79.8 1.5 %collective-permute-done.20.refs_3_ = f32[128,128]{1,0:T(8,128)S(1)} collective-permute-done((f32[128,128]{1,0:T(8,128)S(1)}, f32[128,128]{1,0:T(8,128)S(1)}, u32[]{:S(2)}, u32[]{:S(2)}) %collective-permute-start.20) | collective-permute-done | bytes 65568 | tf_op jit(solution)/shard_map/ppermute | solution.py:329
  81.3 1.1 %collective-permute-done.19.refs_2_ = f32[128,128]{1,0:T(8,128)S(1)} collective-permute-done((f32[128,128]{1,0:T(8,128)S(1)}, f32[128,128]{1,0:T(8,128)S(1)}, u32[]{:S(2)}, u32[]{:S(2)}) %collective-permute-start.19) | collective-permute-done | bytes 65568 | tf_op jit(solution)/shard_map/ppermute | solution.py:329
  82.4 0.0 collective-permute-done.18.refs_1_
  82.4 0.7 shard_map.88
  (6 shorter events, 0.0 us)
Async XLA Ops:
  0.6 15.3 %collective-permute-start.2 = (f32[4,2,128,128]{3,2,1,0:T(8,128)}, f32[4,2,128,128]{3,2,1,0:T(8,128)S(1)}, u32[]{:S(2)}, u32[]{:S(2)}) collective-permute-start(f32[4,2,128,128]{3,2,1,0:T(8,128)} %probe.1), channel_id=1, source_target_pairs={{0,1},{1,0},{2,3},{3,2},{4,5},{5,4},{6,7},{7,6},{8,9},{9,8},{10,11... | collective-permute-start | bytes 1572872 | tf_op jit(solution)/shard_map/ppermute | solution.py:329
  3.7 0.9 %copy-start.3 = (f32[1,2,2,128,128]{4,3,2,1,0:T(8,128)S(1)}, f32[1,2,2,128,128]{4,3,2,1,0:T(8,128)}, u32[]{:S(2)}) copy-start(f32[1,2,2,128,128]{4,3,2,1,0:T(8,128)} %param.6) | copy-start | bytes 786436
  4.8 5.3 %collective-permute-start = (f32[2,128,128]{2,1,0:T(8,128)S(1)}, f32[2,128,128]{2,1,0:T(8,128)S(1)}, u32[]{:S(2)}, u32[]{:S(2)}) collective-permute-start(f32[2,128,128]{2,1,0:T(8,128)S(1)} %get-tuple-element.34), channel_id=1, source_target_pairs={{0,4},{4,8},{8,12},{12,16},{16,20},{20,24},{24,28},{28,0},{1,5},{5... | collective-permute-start | bytes 393224 | tf_op jit(solution)/shard_map/ppermute | solution.py:334
  4.9 5.3 %collective-permute-start.1 = (f32[2,128,128]{2,1,0:T(8,128)S(1)}, f32[2,128,128]{2,1,0:T(8,128)S(1)}, u32[]{:S(2)}, u32[]{:S(2)}) collective-permute-start(f32[2,128,128]{2,1,0:T(8,128)S(1)} %get-tuple-element.35), channel_id=1, source_target_pairs={{0,28},{4,0},{8,4},{12,8},{16,12},{20,16},{24,20},{28,24},{1,29},{... | collective-permute-start | bytes 393224 | tf_op jit(solution)/shard_map/ppermute | solution.py:334
  7.5 1.0 %copy-start.2 = (f32[4,2,128,128]{3,2,1,0:T(8,128)S(1)}, f32[4,2,128,128]{3,2,1,0:T(8,128)}, u32[]{:S(2)}) copy-start(f32[4,2,128,128]{3,2,1,0:T(8,128)} %probe.1) | copy-start | bytes 1572868
  8.6 0.7 copy-start.5
  8.6 0.9 %copy-start.4 = (f32[128,128]{1,0:T(8,128)S(1)}, f32[128,128]{1,0:T(8,128)}, u32[]{:S(2)}) copy-start(f32[128,128]{1,0:T(8,128)} %param.8) | copy-start | bytes 196612
  8.6 1.6 %copy-start = (bf16[2,256,256]{2,1,0:T(8,128)(2,1)S(1)}, bf16[2,256,256]{2,1,0:T(8,128)(2,1)}, u32[]{:S(2)}) copy-start(bf16[2,256,256]{2,1,0:T(8,128)(2,1)} %constant.6.clone.refs_6_.table.refs_9_.refs_7_) | copy-start | bytes 786436
  15.9 7.0 %copy-start.1 = (f32[4,128,128]{2,1,0:T(8,128)S(1)}, f32[4,128,128]{2,1,0:T(8,128)}, u32[]{:S(2)}) copy-start(f32[4,128,128]{2,1,0:T(8,128)} %refs_2_.3) | copy-start | bytes 786436
  17.6 5.2 %collective-permute-start.3 = (f32[128,128]{1,0:T(8,128)S(1)}, f32[128,128]{1,0:T(8,128)S(1)}, u32[]{:S(2)}, u32[]{:S(2)}) collective-permute-start(f32[128,128]{1,0:T(8,128)S(1)} %get-tuple-element.40.refs_0_), channel_id=1, source_target_pairs={{0,2},{1,3},{2,0},{3,1},{4,6},{5,7},{6,4},{7,5},{8,10},{9,11},{10,... | collective-permute-start | bytes 196616 | tf_op jit(solution)/shard_map/ppermute | solution.py:329
  25.7 11.0 %collective-permute-start.4 = (f32[2,128,128]{2,1,0:T(8,128)S(1)}, f32[2,128,128]{2,1,0:T(8,128)S(1)}, u32[]{:S(2)}, u32[]{:S(2)}) collective-permute-start(f32[2,128,128]{2,1,0:T(8,128)S(1)} %get-tuple-element.45.refs_0_), channel_id=1, source_target_pairs={{0,1},{1,0},{2,3},{3,2},{4,5},{5,4},{6,7},{7,6},{8,9},{9,8},{10,11... | collective-permute-start | bytes 393224 | tf_op jit(solution)/shard_map/ppermute | solution.py:329
  27.5 6.0 %collective-permute-start.5 = (f32[128,128]{1,0:T(8,128)S(1)}, f32[128,128]{1,0:T(8,128)S(1)}, u32[]{:S(2)}, u32[]{:S(2)}) collective-permute-start(f32[128,128]{1,0:T(8,128)S(1)} %get-tuple-element.46), channel_id=1, source_target_pairs={{0,2},{1,3},{2,0},{3,1},{4,6},{5,7},{6,4},{7,5},{8,10},{9,11},{10,... | collective-permute-start | bytes 196616 | tf_op jit(solution)/shard_map/ppermute | solution.py:329
  30.7 6.1 %collective-permute-start.6 = (f32[128,128]{1,0:T(8,128)S(1)}, f32[128,128]{1,0:T(8,128)S(1)}, u32[]{:S(2)}, u32[]{:S(2)}) collective-permute-start(f32[128,128]{1,0:T(8,128)S(1)} %get-tuple-element.47), channel_id=1, source_target_pairs={{0,3},{1,2},{2,1},{3,0},{4,7},{5,6},{6,5},{7,4},{8,11},{9,10},{10,... | collective-permute-start | bytes 196616 | tf_op jit(solution)/shard_map/ppermute | solution.py:329
  37.1 2.0 %collective-permute-start.8 = (f32[128,128]{1,0:T(8,128)S(1)}, f32[128,128]{1,0:T(8,128)S(1)}, u32[]{:S(2)}, u32[]{:S(2)}) collective-permute-start(f32[128,128]{1,0:T(8,128)S(1)} %get-tuple-element.48.left), channel_id=1, source_target_pairs={{0,28},{4,0},{8,4},{12,8},{16,12},{20,16},{24,20},{28,24},{1,29},{... | collective-permute-start | bytes 196616 | tf_op jit(solution)/shard_map/ppermute | solution.py:334
  37.1 5.4 %collective-permute-start.7 = (f32[128,128]{1,0:T(8,128)S(1)}, f32[128,128]{1,0:T(8,128)S(1)}, u32[]{:S(2)}, u32[]{:S(2)}) collective-permute-start(f32[128,128]{1,0:T(8,128)S(1)} %get-tuple-element.49.right), channel_id=1, source_target_pairs={{0,4},{4,8},{8,12},{12,16},{16,20},{20,24},{24,28},{28,0},{1,5},{5... | collective-permute-start | bytes 196616 | tf_op jit(solution)/shard_map/ppermute | solution.py:334
  42.8 5.2 %collective-permute-start.10 = (f32[128,128]{1,0:T(8,128)S(1)}, f32[128,128]{1,0:T(8,128)S(1)}, u32[]{:S(2)}, u32[]{:S(2)}) collective-permute-start(f32[128,128]{1,0:T(8,128)S(1)} %get-tuple-element.51.refs_0_), channel_id=1, source_target_pairs={{0,2},{1,3},{2,0},{3,1},{4,6},{5,7},{6,4},{7,5},{8,10},{9,11},{10,... | collective-permute-start | bytes 196616 | tf_op jit(solution)/shard_map/ppermute | solution.py:329
  42.9 6.2 %collective-permute-start.11 = (f32[128,128]{1,0:T(8,128)S(1)}, f32[128,128]{1,0:T(8,128)S(1)}, u32[]{:S(2)}, u32[]{:S(2)}) collective-permute-start(f32[128,128]{1,0:T(8,128)S(1)} %get-tuple-element.52), channel_id=1, source_target_pairs={{0,3},{1,2},{2,1},{3,0},{4,7},{5,6},{6,5},{7,4},{8,11},{9,10},{10,... | collective-permute-start | bytes 196616 | tf_op jit(solution)/shard_map/ppermute | solution.py:329
  44.2 5.2 %collective-permute-start.9 = (f32[128,128]{1,0:T(8,128)S(1)}, f32[128,128]{1,0:T(8,128)S(1)}, u32[]{:S(2)}, u32[]{:S(2)}) collective-permute-start(f32[128,128]{1,0:T(8,128)S(1)} %get-tuple-element.52), channel_id=1, source_target_pairs={{0,1},{1,0},{2,3},{3,2},{4,5},{5,4},{6,7},{7,6},{8,9},{9,8},{10,11... | collective-permute-start | bytes 196616 | tf_op jit(solution)/shard_map/ppermute | solution.py:329
  52.3 5.2 %collective-permute-start.12 = (f32[128,128]{1,0:T(8,128)S(1)}, f32[128,128]{1,0:T(8,128)S(1)}, u32[]{:S(2)}, u32[]{:S(2)}) collective-permute-start(f32[128,128]{1,0:T(8,128)S(1)} %get-tuple-element.53.refs_0_), channel_id=1, source_target_pairs={{0,2},{1,3},{2,0},{3,1},{4,6},{5,7},{6,4},{7,5},{8,10},{9,11},{10,... | collective-permute-start | bytes 196616 | tf_op jit(solution)/shard_map/ppermute | solution.py:329
  60.4 9.1 %collective-permute-start.13 = (f32[2,128,128]{2,1,0:T(8,128)S(1)}, f32[2,128,128]{2,1,0:T(8,128)S(1)}, u32[]{:S(2)}, u32[]{:S(2)}) collective-permute-start(f32[2,128,128]{2,1,0:T(8,128)S(1)} %get-tuple-element.58.refs_2_), channel_id=1, source_target_pairs={{0,1},{1,0},{2,3},{3,2},{4,5},{5,4},{6,7},{7,6},{8,9},{9,8},{10,11... | collective-permute-start | bytes 393224 | tf_op jit(solution)/shard_map/ppermute | solution.py:329
  61.7 5.9 %collective-permute-start.14 = (f32[128,128]{1,0:T(8,128)S(1)}, f32[128,128]{1,0:T(8,128)S(1)}, u32[]{:S(2)}, u32[]{:S(2)}) collective-permute-start(f32[128,128]{1,0:T(8,128)S(1)} %get-tuple-element.59), channel_id=1, source_target_pairs={{0,2},{1,3},{2,0},{3,1},{4,6},{5,7},{6,4},{7,5},{8,10},{9,11},{10,... | collective-permute-start | bytes 196616 | tf_op jit(solution)/shard_map/ppermute | solution.py:329
  63.4 6.1 %collective-permute-start.15 = (f32[128,128]{1,0:T(8,128)S(1)}, f32[128,128]{1,0:T(8,128)S(1)}, u32[]{:S(2)}, u32[]{:S(2)}) collective-permute-start(f32[128,128]{1,0:T(8,128)S(1)} %get-tuple-element.60), channel_id=1, source_target_pairs={{0,3},{1,2},{2,1},{3,0},{4,7},{5,6},{6,5},{7,4},{8,11},{9,10},{10,... | collective-permute-start | bytes 196616 | tf_op jit(solution)/shard_map/ppermute | solution.py:329
  69.8 2.0 %collective-permute-start.17 = (f32[128,128]{1,0:T(8,128)S(1)}, f32[128,128]{1,0:T(8,128)S(1)}, u32[]{:S(2)}, u32[]{:S(2)}) collective-permute-start(f32[128,128]{1,0:T(8,128)S(1)} %get-tuple-element.61.left), channel_id=1, source_target_pairs={{0,28},{4,0},{8,4},{12,8},{16,12},{20,16},{24,20},{28,24},{1,29},{... | collective-permute-start | bytes 196616 | tf_op jit(solution)/shard_map/ppermute | solution.py:334
  69.8 4.6 %collective-permute-start.16 = (f32[128,128]{1,0:T(8,128)S(1)}, f32[128,128]{1,0:T(8,128)S(1)}, u32[]{:S(2)}, u32[]{:S(2)}) collective-permute-start(f32[128,128]{1,0:T(8,128)S(1)} %get-tuple-element.62.right), channel_id=1, source_target_pairs={{0,4},{4,8},{8,12},{12,16},{16,20},{20,24},{24,28},{28,0},{1,5},{5... | collective-permute-start | bytes 196616 | tf_op jit(solution)/shard_map/ppermute | solution.py:334
  74.6 6.7 %collective-permute-start.20 = (f32[128,128]{1,0:T(8,128)S(1)}, f32[128,128]{1,0:T(8,128)S(1)}, u32[]{:S(2)}, u32[]{:S(2)}) collective-permute-start(f32[128,128]{1,0:T(8,128)S(1)} %shard_map.87.refs_0_), channel_id=1, source_target_pairs={{0,3},{1,2},{2,1},{3,0},{4,7},{5,6},{6,5},{7,4},{8,11},{9,10},{10,... | collective-permute-start | bytes 196616 | tf_op jit(solution)/shard_map/ppermute | solution.py:329
  76.3 6.1 %collective-permute-start.19 = (f32[128,128]{1,0:T(8,128)S(1)}, f32[128,128]{1,0:T(8,128)S(1)}, u32[]{:S(2)}, u32[]{:S(2)}) collective-permute-start(f32[128,128]{1,0:T(8,128)S(1)} %shard_map.87.refs_0_), channel_id=1, source_target_pairs={{0,2},{1,3},{2,0},{3,1},{4,6},{5,7},{6,4},{7,5},{8,10},{9,11},{10,... | collective-permute-start | bytes 196616 | tf_op jit(solution)/shard_map/ppermute | solution.py:329
  76.3 6.1 %collective-permute-start.18 = (f32[128,128]{1,0:T(8,128)S(1)}, f32[128,128]{1,0:T(8,128)S(1)}, u32[]{:S(2)}, u32[]{:S(2)}) collective-permute-start(f32[128,128]{1,0:T(8,128)S(1)} %shard_map.87.refs_0_), channel_id=1, source_target_pairs={{0,1},{1,0},{2,3},{3,2},{4,5},{5,4},{6,7},{7,6},{8,9},{9,8},{10,11... | collective-permute-start | bytes 196616 | tf_op jit(solution)/shard_map/ppermute | solution.py:329
